TPU v7x, 256 devices: a whole 4x4x8 slice. The times are simulated.
256 devices in a mesh: wide: 32 (over x, y, z_hi), narrow: 8 (over z_lo, core).
Axes of the slice: x: 4, y: 4, z: 8 (z_hi: 2, z_lo: 4; z = z_hi * 4 + z_lo), core: 2. Of those that a mesh axis runs over, the one named last changes fastest.
Arguments:
- amplitudes: float32 [262144, 128], P(('wide', 'narrow')), may hold values from -6 to 6
- top_gates: float32 [4, 2, 32, 32], replicated, may hold values from -0.32 to 1.21
- mid_gates: float32 [3, 2, 32, 32], replicated, may hold values from -0.32 to 1.21
- low_gates: float32 [3, 2, 64, 64], replicated, may hold values from -0.32 to 1.21
- ham_top: float32 [3, 2, 2, 32, 32], replicated, may hold values from -0.32 to 1.21
- ham_mid: float32 [3, 2, 32, 32], replicated, may hold values from -0.32 to 1.21
- ham_low: float32 [3, 2, 64, 64], replicated, may hold values from -0.32 to 1.21
- flip_masks: int32 [3], replicated, may hold values from 0 to 65535
- phase_masks: int32 [3], replicated, may hold values from 0 to 65535
- device_phase_masks: int32 [3], replicated, may hold values from 0 to 255
Outputs:
- final_state: float32 [262144, 128], P(('wide', 'narrow'))
- cotangent: float32 [262144, 128], P(('wide', 'narrow'))
All inputs are finite; a program needn't handle non-finite values.
Results may differ from a plain program's by a relative error of at most 0.00014.
Values sent between devices are 32-bit elements; how exact they have to be, the bound alone decides.
No kernel may reach another device: no remote copies, remote signals or barrier semaphores. Data moves between devices by JAX's collectives and lax.ppermute only.
A program may use at most 64 MiB of HBM per device.

v0:
```python
import jax
import jax.numpy as jnp
from jax import lax
from jax.sharding import PartitionSpec as P

TOP = 32
MID = 32
LOW = 64
ROUNDS = 3
BLOCKS = 3


HIGH = lax.Precision.HIGHEST


def partner(block, axis, distance):
    count = lax.axis_size(axis)
    route = []
    for low in range(count):
        high = low | 1 << distance
        if high != low and high < count:
            route += [(low, high), (high, low)]
    return lax.ppermute(block, axis, route)


def combine(real_part, imag_part):
    return jnp.stack(
        [real_part[..., 0, :] - imag_part[..., 1, :], real_part[..., 1, :] + imag_part[..., 0, :]],
        axis=-2,
    )


def apply_high(field, matrix):
    height, items, width = field.shape
    flat = field.reshape(height, items * width)
    real_part = jnp.dot(matrix[0], flat, precision=HIGH).reshape(height, items, 2, width // 2)
    imag_part = jnp.dot(matrix[1], flat, precision=HIGH).reshape(height, items, 2, width // 2)
    return combine(real_part, imag_part).reshape(height, items, width)


def apply_mid(field, matrix):
    height, items, width = field.shape
    real_part = jnp.einsum("ij,ajk->aik", matrix[0], field, precision=HIGH).reshape(
        height, items, 2, width // 2
    )
    imag_part = jnp.einsum("ij,ajk->aik", matrix[1], field, precision=HIGH).reshape(
        height, items, 2, width // 2
    )
    return combine(real_part, imag_part).reshape(height, items, width)


def apply_low(field, matrix):
    height, items, width = field.shape
    upper = jnp.concatenate([matrix[0].T, matrix[1].T], axis=1)
    bottom = jnp.concatenate([-matrix[1].T, matrix[0].T], axis=1)
    joined = jnp.concatenate([upper, bottom], axis=0)
    return jnp.dot(field.reshape(height * items, width), joined, precision=HIGH).reshape(
        height, items, width
    )


def parity(values, selector):
    folded = jnp.bitwise_and(values, selector)
    for offset in (16, 8, 4, 2, 1):
        folded = jnp.bitwise_xor(folded, jnp.right_shift(folded, offset))
    odd_bit = jnp.bitwise_and(folded, 1)
    return (1 - 2 * odd_bit).astype(jnp.float32)


def fold_rows(matrix, flip_digit, phase_digit):
    row_ids = jnp.arange(matrix.shape[1], dtype=jnp.int32)
    source = jnp.bitwise_xor(row_ids, flip_digit)
    signs = parity(source, phase_digit)
    return jnp.take(matrix, source, axis=1) * signs[None, :, None]


def shards(
    amplitudes,
    top_gates,
    mid_gates,
    low_gates,
    ham_top,
    ham_mid,
    ham_low,
    flip_masks,
    phase_masks,
    device_phase_masks,
):
    wide_count = lax.axis_size("wide")
    narrow_count = lax.axis_size("narrow")
    a_rest = TOP // wide_count
    width = 2 * LOW
    current = amplitudes.reshape(TOP, MID, width)
    inside = lax.all_to_all(
        current.reshape(wide_count, a_rest, MID, width),
        "wide",
        split_axis=0,
        concat_axis=0,
        tiled=True,
    ).reshape(TOP, MID, width)

    def plain_round(round_id, field):
        field = apply_high(field, top_gates[round_id])
        field = apply_mid(field, mid_gates[round_id])
        return apply_low(field, low_gates[round_id])

    inside = lax.fori_loop(0, ROUNDS, plain_round, inside)
    inside = apply_high(inside, top_gates[ROUNDS])
    current = lax.all_to_all(
        inside.reshape(wide_count, a_rest, MID, width),
        "wide",
        split_axis=0,
        concat_axis=0,
        tiled=True,
    ).reshape(TOP, MID, width)
    final_state = current.reshape(TOP * MID, width)
    device_id = lax.axis_index("wide") * narrow_count + lax.axis_index("narrow")
    results = []
    for block_id in range(BLOCKS):
        flip = flip_masks[block_id]
        phase = phase_masks[block_id]
        last_high = fold_rows(ham_top[block_id, 1], flip // (MID * LOW), phase // (MID * LOW))
        middle = fold_rows(ham_mid[block_id], flip // LOW % MID, phase // LOW % MID)
        lowest = fold_rows(ham_low[block_id], flip % LOW, phase % LOW)
        result = apply_high(current, ham_top[block_id, 0])
        result = apply_mid(result, middle)
        result = apply_low(result, lowest)
        result = apply_high(result, last_high)
        results.append(result * parity(device_id, device_phase_masks[block_id]))
    wide_bit = wide_count.bit_length() - 2
    narrow_bit = narrow_count.bit_length() - 2
    paired = partner(jnp.stack([results[0], results[2]]), "wide", wide_bit)
    joint = partner(results[1] + paired[1], "narrow", narrow_bit)
    total = paired[0] + joint
    cotangent = total.reshape(TOP * MID, width)
    return (final_state, cotangent)


def solution(mesh):
    return jax.shard_map(
        shards,
        mesh=mesh,
        in_specs=(P(("wide", "narrow"), None), P(), P(), P(), P(), P(), P(), P(), P(), P()),
        out_specs=(P(("wide", "narrow"), None), P(("wide", "narrow"), None)),
        check_vma=False,
    )
```

profile of v0, /device:TPU:1, one launch (start us, length us, event | category | flops | bytes accessed | tf_op | source)
XLA Modules:
  0.0 256.3 jit_solution(6728141692377350689)
XLA Ops:
  0.6 14.5 %all-to-all-start = ((f32[32,1,32,128]{3,2,1,0:T(8,128)}), f32[32,1,32,128]{3,2,1,0:T(8,128)S(1)}, u32[]{:S(2)}, u32[]{:S(2)}) async-start(f32[32,1,32,128]{3,2,1,0:T(8,128)} %bitcast.341), calls=%async_computation | async-start | bytes 1048576 | tf_op jit(solution)/shard_map/all_to_all | solution.py:94
  47.8 43.4 %while.13 = (s32[]{:T(128)}, f32[32,32,128]{2,1,0:T(8,128)S(1)}, f32[4,2,32,32]{3,2,1,0:T(8,128)S(1)}, f32[3,2,32,32]{3,2,1,0:T(8,128)}, f32[3,2,64,64]{3,2,1,0:T(8,128)}, /*index=5*/s32[]{:T(128)}, s32[]{:T(128)}, s32[]{}) while((s32[]{:T(128)}, f32[32,32,128]{2,1,0:T(8,128)S(1)}, f32[4,2,32,32]{3,2,1,0:T(8,128)S(1)}, ...), condition=%wide.region_1.0_spmd, body=%wide.region_0.0_spmd.sunk | while | flops 403230720 | bytes 19154040 | solution.py:107
  49.0 1.6 fusion.159
  50.6 1.6 fusion.160
  53.9 1.3 convolution_bitcast_fusion.18
  55.8 1.3 convolution_bitcast_fusion.19
  57.7 1.1 slice_subtract_fusion.15
  58.9 1.2 pad_maximum_fusion.13
  63.4 1.6 fusion.159
  64.9 1.6 fusion.160
  68.2 1.3 convolution_bitcast_fusion.18
  70.2 1.3 convolution_bitcast_fusion.19
  72.1 1.1 slice_subtract_fusion.15
  73.2 1.2 pad_maximum_fusion.13
  77.7 1.6 fusion.159
  79.3 1.6 fusion.160
  82.6 1.3 convolution_bitcast_fusion.18
  84.5 1.3 convolution_bitcast_fusion.19
  86.4 1.1 slice_subtract_fusion.15
  87.5 1.2 pad_maximum_fusion.13
  95.6 1.2 pad_maximum_fusion.2
  96.9 1.4 reshape_reshape.33
  98.3 12.0 %all-to-all-start.1 = ((f32[32,1,32,128]{3,2,1,0:T(8,128)}), f32[32,1,32,128]{3,2,1,0:T(8,128)S(1)}, u32[]{:S(2)}, u32[]{:S(2)}) async-start(f32[32,1,32,128]{3,2,1,0:T(8,128)} %reshape_reshape.33), calls=%async_computation.1 | async-start | bytes 1048576 | tf_op jit(solution)/shard_map/all_to_all | solution.py:109
  116.2 8.6 %all-to-all-done.1 = f32[32,1,32,128]{3,2,1,0:T(8,128)S(1)} async-done(((f32[32,1,32,128]{3,2,1,0:T(8,128)}), f32[32,1,32,128]{3,2,1,0:T(8,128)S(1)}, u32[]{:S(2)}, u32[]{:S(2)}) %all-to-all-start.1) | async-done | bytes 524320 | tf_op jit(solution)/shard_map/all_to_all | solution.py:109
  124.8 1.6 convolution_bitcast_fusion.7
  126.4 1.6 convolution_bitcast_fusion.6
  129.6 1.1 slice_subtract_fusion.10
  130.7 1.2 pad_maximum_fusion.3
  136.0 1.2 pad_maximum_fusion.4
  139.5 1.6 fusion.26
  141.1 2.6 %fusion.24 = f32[32,32,2,64]{3,0,2,1:T(8,128)} fusion(f32[32,2,64,32]{2,1,0,3:T(2,128)S(1)} %dot_general.144, f32[2,32,32]{2,1,0:T(8,128)S(1)} %bitcast_multiply_fusion.8), kind=kOutput, calls=%fused_computation.75 | convolution fusion | flops 50331648 | bytes 1589248 | tf_op jit(solution)/shard_map/dot_general | solution.py:37
  143.7 2.4 convolution_bitcast_fusion.5
  146.1 1.6 convolution_bitcast_fusion.4
  147.8 1.8 reshape.373
  149.6 1.8 reshape.374
  151.3 3.1 %slice_subtract_fusion.7 = (f32[32,32,1,64]{3,2,1,0:T(1,128)S(1)}, f32[32,32,1,64]{3,2,1,0:T(1,128)S(1)}) fusion(f32[32,32,2,64]{3,2,1,0:T(2,128)} %reshape.374, f32[32,32,2,64]{3,2,1,0:T(2,128)S(1)} %reshape.373), kind=kLoop, calls=%fused_computation.102 | loop fusion | flops 131072 | bytes 1572864 | tf_op jit(solution)/shard_map/sub | solution.py:28
  154.4 1.2 pad_maximum_fusion.5
  156.2 1.6 convolution_bitcast_fusion.13
  158.4 1.7 reshape.376
  160.0 1.6 reshape.377
  161.7 3.1 %slice_subtract_fusion.6 = (f32[32,32,1,64]{3,2,1,0:T(1,128)S(1)}, f32[32,32,1,64]{3,2,1,0:T(1,128)S(1)}) fusion(f32[32,32,2,64]{3,2,1,0:T(2,128)} %reshape.377, f32[32,32,2,64]{3,2,1,0:T(2,128)S(1)} %reshape.376), kind=kLoop, calls=%fused_computation.100 | loop fusion | flops 131072 | bytes 1572864 | tf_op jit(solution)/shard_map/sub | solution.py:28
  164.8 1.2 pad_maximum_fusion.6
  168.3 2.6 %fusion.22 = f32[32,32,2,64]{3,0,2,1:T(8,128)} fusion(f32[32,2,64,32]{2,1,0,3:T(2,128)S(1)} %dot_general.155, f32[2,32,32]{2,1,0:T(8,128)S(1)} %bitcast_multiply_fusion.6), kind=kOutput, calls=%fused_computation.73 | convolution fusion | flops 50331648 | bytes 1589248 | tf_op jit(solution)/shard_map/dot_general | solution.py:36
  170.8 2.5 fusion.20
  173.4 2.4 convolution_bitcast_fusion.3
  175.8 1.6 convolution_bitcast_fusion.2
  177.4 2.2 reshape.378
  179.6 1.7 reshape.379
  181.4 3.0 %slice_subtract_fusion.4 = (f32[32,32,1,64]{3,2,1,0:T(1,128)S(1)}, f32[32,32,1,64]{3,2,1,0:T(1,128)S(1)}) fusion(f32[32,32,2,64]{3,2,1,0:T(2,128)} %reshape.379, f32[32,32,2,64]{3,2,1,0:T(2,128)S(1)} %reshape.378), kind=kLoop, calls=%fused_computation.94 | loop fusion | flops 131072 | bytes 1572864 | tf_op jit(solution)/shard_map/sub | solution.py:28
  184.4 1.2 pad_maximum_fusion.8
  186.2 1.4 convolution_bitcast_fusion.11
  188.5 1.8 copy.56
  190.4 2.7 %mul.201 = f32[1,32,32,128]{3,2,1,0:T(8,128)} reshape(f32[32,32,2,64]{3,2,1,0:T(2,128)} %copy.56) | data formatting | bytes 1048576 | tf_op jit(solution)/shard_map/mul | solution.py:129
  194.2 1.4 mul.214
  195.6 2.2 pad_maximum_fusion.7
  199.7 1.1 slice_subtract_fusion.3
  200.8 1.2 pad_maximum_fusion.9
  204.3 1.6 fusion.18
  205.9 1.6 fusion.16
  209.2 11.8 %collective-permute-done = f32[2,32,32,128]{3,2,1,0:T(8,128)} collective-permute-done((f32[2,32,32,128]{3,2,1,0:T(8,128)}, f32[2,32,32,128]{3,2,1,0:T(8,128)}, u32[]{:S(2)}, u32[]{:S(2)}) %collective-permute-start) | collective-permute-done | bytes 1048608 | tf_op jit(solution)/shard_map/ppermute | solution.py:23
  221.0 1.1 fusion.36
  222.1 9.2 %collective-permute-start.1 = (f32[32,32,128]{2,1,0:T(8,128)S(1)}, f32[32,32,128]{2,1,0:T(8,128)S(1)}, u32[]{:S(2)}, u32[]{:S(2)}) collective-permute-start(f32[32,32,128]{2,1,0:T(8,128)S(1)} %fusion.36), channel_id=1, source_target_pairs={{0,4},{4,0},{1,5},{5,1},{2,6},{6,2},{3,7},{7,3},{8,12},{12,8},{9,1... | collective-permute-start | bytes 1572872 | tf_op jit(solution)/shard_map/ppermute | solution.py:23
  231.3 22.0 %collective-permute-done.1 = f32[32,32,128]{2,1,0:T(8,128)S(1)} collective-permute-done((f32[32,32,128]{2,1,0:T(8,128)S(1)}, f32[32,32,128]{2,1,0:T(8,128)S(1)}, u32[]{:S(2)}, u32[]{:S(2)}) %collective-permute-start.1) | collective-permute-done | bytes 524320 | tf_op jit(solution)/shard_map/ppermute | solution.py:23
  253.4 1.9 fusion.37
  (200 shorter events, 64.1 us)
Async XLA Ops:
  0.6 14.5 %copy-start.16 = (s32[3]{0:T(128)S(1)}, s32[3]{0:T(128)}, u32[]{:S(2)}) copy-start(s32[3]{0:T(128)} %param.23) | copy-start | bytes 40
  0.6 47.1 %all-to-all-start = ((f32[32,1,32,128]{3,2,1,0:T(8,128)}), f32[32,1,32,128]{3,2,1,0:T(8,128)S(1)}, u32[]{:S(2)}, u32[]{:S(2)}) async-start(f32[32,1,32,128]{3,2,1,0:T(8,128)} %bitcast.341), calls=%async_computation | async-start | bytes 1048576 | tf_op jit(solution)/shard_map/all_to_all | solution.py:94
  18.4 0.7 copy-start.17
  25.6 7.2 %copy-start.15 = (f32[3,2,32,32]{3,2,1,0:T(8,128)S(1)}, f32[3,2,32,32]{3,2,1,0:T(8,128)}, u32[]{:S(2)}) copy-start(f32[3,2,32,32]{3,2,1,0:T(8,128)} %param.21) | copy-start | bytes 73732
  30.3 2.6 %copy-start.7 = (f32[3,2,64,64]{3,2,1,0:T(8,128)S(1)}, f32[3,2,64,64]{3,2,1,0:T(8,128)}, u32[]{:S(2)}) copy-start(f32[3,2,64,64]{3,2,1,0:T(8,128)} %param.22) | copy-start | bytes 294916
  33.7 0.9 copy-start.6
  34.7 0.7 copy-start.18
  46.4 1.4 copy-start.5
  96.9 13.4 %copy-start.13 = (f32[2,32,32]{2,0,1:T(2,128)S(1)}, f32[2,32,32]{2,0,1:T(2,128)}, u32[]{:S(2)}) copy-start(f32[2,32,32]{2,0,1:T(2,128)} %get-tuple-element.175) | copy-start | bytes 24580
  98.3 26.5 %all-to-all-start.1 = ((f32[32,1,32,128]{3,2,1,0:T(8,128)}), f32[32,1,32,128]{3,2,1,0:T(8,128)S(1)}, u32[]{:S(2)}, u32[]{:S(2)}) async-start(f32[32,1,32,128]{3,2,1,0:T(8,128)} %reshape_reshape.33), calls=%async_computation.1 | async-start | bytes 1048576 | tf_op jit(solution)/shard_map/all_to_all | solution.py:109
  110.3 0.8 copy-start.14
  111.1 0.8 copy-start.11
  111.8 0.8 copy-start.12
  113.2 0.7 copy-start.19
  113.2 0.7 copy-start.23
  113.9 0.7 copy-start.20
  113.9 0.7 copy-start.24
  114.7 0.6 copy-start.21
  114.7 0.7 copy-start.25
  115.5 0.7 copy-start.22
  137.2 0.8 copy-start.8
  166.0 0.8 copy-start.9
  186.2 2.0 copy-start
  188.5 4.6 %copy-start.2 = (f32[32,32,2,64]{3,0,2,1:T(8,128)S(1)}, f32[32,32,2,64]{3,0,2,1:T(8,128)}, u32[]{:S(2)}) copy-start(f32[32,32,2,64]{3,0,2,1:T(8,128)} %fusion.20) | copy-start | bytes 1572868
  190.4 2.7 %copy-start.1 = (f32[32,32,2,64]{3,0,2,1:T(8,128)S(1)}, f32[32,32,2,64]{3,0,2,1:T(8,128)}, u32[]{:S(2)}) copy-start(f32[32,32,2,64]{3,0,2,1:T(8,128)} %fusion.22) | copy-start | bytes 1572868
  194.2 1.4 copy-start.4
  195.6 2.8 %copy-start.3 = (f32[32,32,128]{2,1,0:T(8,128)S(1)}, f32[32,32,128]{2,1,0:T(8,128)}, u32[]{:S(2)}) copy-start(f32[32,32,128]{2,1,0:T(8,128)} %convolution_bitcast_fusion.11) | copy-start | bytes 1572868
  197.8 23.2 %collective-permute-start = (f32[2,32,32,128]{3,2,1,0:T(8,128)}, f32[2,32,32,128]{3,2,1,0:T(8,128)}, u32[]{:S(2)}, u32[]{:S(2)}) collective-permute-start(f32[2,32,32,128]{3,2,1,0:T(8,128)} %pad_maximum_fusion.7), channel_id=1, source_target_pairs={{0,128},{128,0},{8,136},{136,8},{16,144},{144,16},{24,152},{152,24... | collective-permute-start | bytes 3145736 | tf_op jit(solution)/shard_map/ppermute | solution.py:23
  202.0 0.8 copy-start.10
  222.1 31.2 %collective-permute-start.1 = (f32[32,32,128]{2,1,0:T(8,128)S(1)}, f32[32,32,128]{2,1,0:T(8,128)S(1)}, u32[]{:S(2)}, u32[]{:S(2)}) collective-permute-start(f32[32,32,128]{2,1,0:T(8,128)S(1)} %fusion.36), channel_id=1, source_target_pairs={{0,4},{4,0},{1,5},{5,1},{2,6},{6,2},{3,7},{7,3},{8,12},{12,8},{9,1... | collective-permute-start | bytes 1572872 | tf_op jit(solution)/shard_map/ppermute | solution.py:23
where the time goes:
time: 261 us; the launch traced here: 256 us
  local copies, waits for them, and re-layouts  64.2 us (25%)
  matrix products  51.9 us (20%)
  waiting for transfers between devices  42.4 us (16%)
  other arithmetic  41.4 us (16%)
  starting transfers between devices  36.4 us (14%)
  between operations  19.2 us (7%)
    ppermute x2, waiting for transfers between devices, partner(): return lax.ppermute(block, axis, route)  33.8 us
    sub x16, other arithmetic, combine(): real_part[..., 0, :] - imag_part[..., 1, :]  18.2 us
    dot_general x10, matrix products, apply_high(): jnp.dot(matrix[0], flat, precision=HIGH)  17.8 us
    dot_general x10, matrix products, apply_high(): jnp.dot(matrix[1], flat, precision=HIGH)  17.2 us
    all_to_all x1, starting transfers between devices, shards(): lax.all_to_all(current.reshape(wide_count, a_rest, MID, width), 'wide', s...  14.5 us
    another operation x13, other arithmetic, combine(): jnp.stack([real_part[..., 0, :] - imag_part[..., 1, :], real_part[..., 1,...  12.3 us
    all_to_all x1, starting transfers between devices, shards(): lax.all_to_all(inside.reshape(wide_count, a_rest, MID, width), 'wide', sp...  12 us
    ppermute x2, starting transfers between devices, partner(): return lax.ppermute(block, axis, route)  9.85 us
  transfers between devices with their start and end apart: 4, of which 3 were waited for; matrix products, arithmetic and copies ran while one was open for 10% of the time, Pallas kernels for 0%

commit v1 on v0

v1 whole, which is shorter than its diff:
```python
from functools import partial

import jax
import jax.numpy as jnp
from jax import lax
from jax.experimental import pallas as pl
from jax.experimental.pallas import tpu as pltpu
from jax.sharding import Mesh, PartitionSpec as P

TOP = 32
MID = 32
LOW = 64
ROUNDS = 3
BLOCKS = 3
XY = 16
HIGH = lax.Precision.HIGHEST
F32 = jnp.float32
BF16 = jnp.bfloat16


def split(value):
    high = value.astype(BF16)
    return high, (value - high.astype(F32)).astype(BF16)


def dot3(left, right):
    mul = partial(jnp.dot, preferred_element_type=F32)
    return mul(left[0], right[0]) + mul(left[1], right[0]) + mul(left[0], right[1])


def times_i(value):
    lane = lax.broadcasted_iota(jnp.int32, value.shape, 1)
    turned = pltpu.roll(value, LOW, 1)
    return jnp.where(lane < LOW, -turned, turned)


def iotas(shape):
    return lax.broadcasted_iota(jnp.int32, shape, 0), lax.broadcasted_iota(jnp.int32, shape, 1)


def sign_of(bits):
    for offset in (8, 4, 2, 1):
        bits = jnp.bitwise_xor(bits, jnp.right_shift(bits, offset))
    return (1 - 2 * jnp.bitwise_and(bits, 1)).astype(F32)


def hdot(left, right):
    return jnp.dot(left, right, precision=HIGH, preferred_element_type=F32)


def fold_left(order, flip, phase):
    row, col = iotas((order, order))
    return jnp.where(col == jnp.bitwise_xor(row, flip), sign_of(jnp.bitwise_and(col, phase)), 0.0)


def fold_right(order, flip, phase):
    row, col = iotas((order, order))
    return jnp.where(row == jnp.bitwise_xor(col, flip), sign_of(jnp.bitwise_and(row, phase)), 0.0)


def put(ref, index, value):
    high, low = split(value)
    ref[index, 0] = high
    ref[index, 1] = low


def prep_top(small_ref, where_ref, top_ref):
    zh = where_ref[1]
    total = hdot(hdot(small_ref[3], small_ref[2]), hdot(small_ref[1], small_ref[0]))
    row, col = iotas((TOP, 8 * XY))
    in_pick = jnp.where(row == 2 * (col // 8) + zh, 1.0, 0.0)
    wide = hdot(total[:, :TOP], in_pick)
    row, col = iotas((8 * XY, 8 * XY))
    same = jnp.where(row % 8 == col % 8, 1.0, 0.0)
    row, col = iotas((8 * XY, TOP))
    for index in range(2):
        pick = jnp.where(col == 2 * (row // 8) + (zh if index == 0 else 1 - zh), 1.0, 0.0)
        put(
            top_ref,
            index,
            jnp.concatenate([hdot(pick, wide[:TOP]) * same, hdot(pick, wide[TOP:]) * same], axis=1),
        )


def spread_high(matrix, scale):
    row, col = iotas((TOP, 8 * TOP))
    wide = hdot(matrix[:, :TOP], jnp.where(row == col // 8, 1.0, 0.0))
    row, col = iotas((8 * TOP, TOP))
    pick = jnp.where(col == row // 8, 1.0, 0.0)
    row, col = iotas((8 * TOP, 8 * TOP))
    same = jnp.where(row % 8 == col % 8, scale, 0.0)
    return jnp.concatenate([hdot(pick, wide[:TOP]) * same, hdot(pick, wide[TOP:]) * same], axis=1)


def spread_mid(matrix):
    row, col = iotas((MID, 4 * MID))
    wide = hdot(matrix[:, :MID], jnp.where(row == col % MID, 1.0, 0.0))
    row, col = iotas((4 * MID, MID))
    pick = jnp.where(col == row % MID, 1.0, 0.0)
    row, col = iotas((4 * MID, 4 * MID))
    same = jnp.where(row // MID == col // MID, 1.0, 0.0)
    return jnp.concatenate([hdot(pick, wide[:MID]) * same, hdot(pick, wide[MID:]) * same], axis=1)


def prep_blocks(small_ref, large_ref, masks_ref, where_ref, high_ref, mid_ref, low_ref):
    mid = hdot(hdot(small_ref[6], small_ref[5]), small_ref[4])
    low = hdot(hdot(large_ref[0], large_ref[1]), large_ref[2])
    put(mid_ref, BLOCKS, spread_mid(mid))
    put(low_ref, BLOCKS, jnp.concatenate([low, times_i(low)], axis=1))
    for block in range(BLOCKS):
        flip, phase = masks_ref[block], masks_ref[BLOCKS + block]
        source = where_ref[0] if block == 1 else jnp.bitwise_xor(where_ref[0], where_ref[2])
        scale = sign_of(jnp.bitwise_and(source, masks_ref[2 * BLOCKS + block]))
        fold = fold_left(2 * TOP, flip // (MID * LOW), phase // (MID * LOW))
        high = hdot(fold, hdot(small_ref[8 + 2 * block], small_ref[7 + 2 * block]))
        put(high_ref, block, spread_high(high, scale))
        fold = fold_left(2 * MID, flip // LOW % MID, phase // LOW % MID)
        put(mid_ref, block, spread_mid(hdot(fold, hdot(small_ref[13 + block], mid))))
        fold = fold_right(2 * LOW, flip % LOW, phase % LOW)
        full = hdot(hdot(low, large_ref[3 + block]), fold)
        put(low_ref, block, jnp.concatenate([full, times_i(full)], axis=1))


def top_kernel(field_ref, top_ref, own_ref, other_ref):
    for rest in range(2):
        for pair in range(2):
            parts = [
                field_ref[:, rest, 16 * pair + 8 * half : 16 * pair + 8 * half + 8, :].reshape(8 * XY, 2 * LOW)
                for half in range(2)
            ]
            right = jnp.concatenate(
                [jnp.concatenate(parts, axis=1), jnp.concatenate([times_i(part) for part in parts], axis=1)], axis=0
            )
            right = split(right)
            for index, out_ref in enumerate((own_ref, other_ref)):
                done = dot3((top_ref[index, 0], top_ref[index, 1]), right)
                for half in range(2):
                    out_ref[:, rest, 16 * pair + 8 * half : 16 * pair + 8 * half + 8, :] = done[
                        :, 2 * LOW * half : 2 * LOW * (half + 1)
                    ].reshape(XY, 8, 2 * LOW)


def add_kernel(own_ref, got_ref, out_ref):
    half = XY // 2
    total = own_ref[...] + got_ref[...]
    out_ref[:, 0] = total
    out_ref[:half, 1] = total[half:]
    out_ref[half:, 1] = total[:half]


def low_mid(load, mid, low, store):
    for group in range(4):
        done = dot3(split(load(group)), low)
        same, turned = done[:, : 2 * LOW], done[:, 2 * LOW :]
        right = jnp.concatenate(
            [
                jnp.concatenate([same[: 4 * MID], same[4 * MID :]], axis=1),
                jnp.concatenate([turned[: 4 * MID], turned[4 * MID :]], axis=1),
            ],
            axis=0,
        )
        done = dot3(mid, split(right))
        store(group, jnp.concatenate([done[:, : 2 * LOW], done[:, 2 * LOW :]], axis=0))


def pair_of(ref, index):
    return ref[index, 0], ref[index, 1]


def high_step(sources, matrices, out_ref):
    for pair in range(2):
        total = None
        for source_ref, matrix in zip(sources, matrices):
            parts = [
                source_ref[:, 16 * pair + 8 * half : 16 * pair + 8 * half + 8, :].reshape(8 * TOP, 2 * LOW)
                for half in range(2)
            ]
            right = jnp.concatenate(
                [jnp.concatenate(parts, axis=1), jnp.concatenate([times_i(part) for part in parts], axis=1)], axis=0
            )
            done = dot3(matrix, split(right))
            total = done if total is None else total + done
        for half in range(2):
            out_ref[:, 16 * pair + 8 * half : 16 * pair + 8 * half + 8, :] = total[
                :, 2 * LOW * half : 2 * LOW * (half + 1)
            ].reshape(TOP, 8, 2 * LOW)


def reader(field_ref, stream):
    return lambda group: field_ref[4 * group : 4 * group + 4, stream].reshape(8 * MID, 2 * LOW)


def writer(ref):
    def store(group, value):
        ref[8 * group : 8 * group + 8] = value.reshape(8, MID, 2 * LOW)

    return store


def send_kernel(field_ref, high_ref, mid_ref, low_ref, out_ref, first_ref, second_ref):
    low_mid(reader(field_ref, 0), pair_of(mid_ref, 1), pair_of(low_ref, 1), writer(first_ref))
    low_mid(reader(field_ref, 1), pair_of(mid_ref, 2), pair_of(low_ref, 2), writer(second_ref))
    high_step((first_ref, second_ref), (pair_of(high_ref, 1), pair_of(high_ref, 2)), out_ref)


def keep_kernel(field_ref, high_ref, mid_ref, low_ref, final_ref, out_ref, first_ref):
    low_mid(reader(field_ref, 1), pair_of(mid_ref, 0), pair_of(low_ref, 0), writer(first_ref))
    high_step((first_ref,), (pair_of(high_ref, 0),), out_ref)
    low_mid(reader(field_ref, 0), pair_of(mid_ref, 3), pair_of(low_ref, 3), writer(final_ref))


def real_form(matrix):
    real, imag = matrix[:, 0], matrix[:, 1]
    return jnp.concatenate(
        [jnp.concatenate([real, -imag], axis=2), jnp.concatenate([imag, real], axis=2)], axis=1
    )


def flat_form(matrix):
    real, imag = jnp.swapaxes(matrix[:, 0], 1, 2), jnp.swapaxes(matrix[:, 1], 1, 2)
    return jnp.concatenate(
        [jnp.concatenate([real, imag], axis=2), jnp.concatenate([-imag, real], axis=2)], axis=1
    )


def vm():
    return pl.BlockSpec(memory_space=pltpu.VMEM)


def sm():
    return pl.BlockSpec(memory_space=pltpu.SMEM)


def call(body, ins, outs, scratch=(), smem=(), name=None):
    return pl.pallas_call(
        body,
        in_specs=[sm() if i in smem else vm() for i in range(ins)],
        out_specs=[vm() for _ in outs],
        out_shape=[jax.ShapeDtypeStruct(s, t) for s, t in outs],
        scratch_shapes=[pltpu.VMEM(s, t) for s, t in scratch],
        compiler_params=pltpu.CompilerParams(vmem_limit_bytes=48 * 2**20),
        name=name,
    )


def shards(
    amplitudes,
    top_gates,
    mid_gates,
    low_gates,
    ham_top,
    ham_mid,
    ham_low,
    flip_masks,
    phase_masks,
    device_phase_masks,
):
    width = 2 * LOW
    inside = lax.all_to_all(
        amplitudes.reshape(XY, 2 * MID, width), ("x", "y"), split_axis=0, concat_axis=0, tiled=True
    ).reshape(XY, 2, MID, width)
    small = real_form(
        jnp.concatenate([top_gates, mid_gates, ham_top.reshape(2 * BLOCKS, 2, TOP, TOP), ham_mid], axis=0)
    )
    large = flat_form(jnp.concatenate([low_gates, ham_low], axis=0))
    zh = lax.axis_index("zh")
    n = lax.axis_index("narrow")
    device_id = ((lax.axis_index("x") * 4 + lax.axis_index("y")) * 2 + zh) * 8 + n
    where = jnp.stack([device_id, zh, jnp.int32(16 * 8)]).astype(jnp.int32)
    masks = jnp.concatenate([flip_masks, phase_masks, device_phase_masks])
    (top,) = call(prep_top, 2, [((2, 2, 128, 256), BF16)], smem=(1,), name="prep_top")(small, where)
    high, mid, low = call(
        prep_blocks,
        4,
        [((3, 2, 256, 512), BF16), ((4, 2, 128, 256), BF16), ((4, 2, 128, 256), BF16)],
        smem=(2, 3),
        name="prep_blocks",
    )(small, large, masks, where)
    piece = ((XY, 2, MID, width), F32)
    own, other = call(top_kernel, 2, [piece, piece], name="top")(inside, top)
    got = lax.ppermute(other, "zh", [(0, 1), (1, 0)])
    (both,) = call(add_kernel, 2, [((XY, 2, 2, MID, width), F32)], name="add")(own, got)
    field = lax.all_to_all(
        both.reshape(XY, 4 * MID, width), ("x", "y"), split_axis=0, concat_axis=0, tiled=True
    ).reshape(XY, 2, 2, MID, width)
    whole = ((TOP, MID, width), F32)
    (sent,) = call(send_kernel, 4, [whole], [whole, whole], name="send")(field, high, mid, low)
    arrived = lax.ppermute(sent, "narrow", [(i, i ^ 4) for i in range(8)])
    final, kept = call(keep_kernel, 4, [whole, whole], [whole], name="keep")(field, high, mid, low)
    cotangent = kept + arrived
    return final.reshape(TOP * MID, width), cotangent.reshape(TOP * MID, width)


def solution(mesh):
    fine = Mesh(mesh.devices.reshape(4, 4, 2, 8), ("x", "y", "zh", "narrow"))
    rows = P(("x", "y", "zh", "narrow"), None)
    return jax.shard_map(
        shards,
        mesh=fine,
        in_specs=(rows, P(), P(), P(), P(), P(), P(), P(), P(), P()),
        out_specs=(rows, rows),
        check_vma=False,
    )
```

time: 261 us -> 102 us (0.39); the launches traced: 256 us -> 101 us
  local copies, waits for them, and re-layouts: 64.2 us -> 4.88 us
  matrix products: 51.9 us -> 0 us
  other arithmetic: 41.4 us -> 2.51 us
  Pallas kernels: 0 us -> 19.2 us
  between operations: 19.2 us -> 0.81 us
  starting transfers between devices: 36.4 us -> 31.7 us
    dot_general x38 -> x0, matrix products: 51.9 us -> none  [the longest x10 17.8 us: apply_high(): jnp.dot(matrix[0], flat, precision=HIGH)]
    reshape x26 -> x0, local copies, waits for them, and re-layouts: 23.4 us -> none  [the longest x4 5.53 us: apply_high(): jnp.dot(matrix[0], flat, precision=HIGH)]
    pallas_call x0 -> x6, Pallas kernels: none -> 19.2 us  [the longest x1 6.67 us: shards(): call(prep_blocks, 4, [((3, 2, 256, 512), BF16), ((4, 2, 128, 256), BF16),...]
    sub x16 -> x0, other arithmetic: 18.2 us -> none  [combine(): real_part[..., 0, :] - imag_part[..., 1, :]]
    all_to_all x2, starting transfers between devices: 26.5 us -> 11.5 us  [the longest x1 7.58 us: shards(): lax.all_to_all(amplitudes.reshape(XY, 2 * MID, width), ('x', 'y'), split_...]
    another operation x14 -> x1, other arithmetic: 14.5 us -> 0.08 us  [shards(): where = jnp.stack([device_id, zh, jnp.int32(16 * 8)]).astype(jnp.int32)]
    ppermute x2, starting transfers between devices: 9.85 us -> 20.2 us  [the longest x1 13.3 us: shards(): arrived = lax.ppermute(sent, 'narrow', [(i, i ^ 4) for i in range(8)])]
    mul x6 -> x0, local copies, waits for them, and re-layouts: 8.13 us -> none  [shards(): results.append(result * parity(device_id, device_phase_masks[block_id]))]
  transfers between devices with their start and end apart: 4 -> 4, of which waited for: 3 -> 4; matrix products, arithmetic and copies ran while one was open for 10% -> 3% of each run, Pallas kernels for 0% -> 13%
where the time goes in v1:
time: 102 us; the launch traced here: 101 us
  waiting for transfers between devices  42 us (41%)
  starting transfers between devices  31.7 us (31%)
  Pallas kernels  19.2 us (19%)
  local copies, waits for them, and re-layouts  4.88 us (5%)
  other arithmetic  2.51 us (2%)
    ppermute x1, waiting for transfers between devices, shards(): arrived = lax.ppermute(sent, 'narrow', [(i, i ^ 4) for i in range(8)])  17.6 us
    ppermute x1, starting transfers between devices, shards(): arrived = lax.ppermute(sent, 'narrow', [(i, i ^ 4) for i in range(8)])  13.3 us
    ppermute x1, waiting for transfers between devices, shards(): got = lax.ppermute(other, 'zh', [(0, 1), (1, 0)])  12.3 us
    all_to_all x1, starting transfers between devices, shards(): lax.all_to_all(amplitudes.reshape(XY, 2 * MID, width), ('x', 'y'), split_...  7.58 us
    ppermute x1, starting transfers between devices, shards(): got = lax.ppermute(other, 'zh', [(0, 1), (1, 0)])  7 us
    pallas_call x1, Pallas kernels, shards(): call(prep_blocks, 4, [((3, 2, 256, 512), BF16), ((4, 2, 128, 256), BF16),...  6.67 us
    all_to_all x1, waiting for transfers between devices, shards(): lax.all_to_all(amplitudes.reshape(XY, 2 * MID, width), ('x', 'y'), split_...  6.58 us
    all_to_all x1, waiting for transfers between devices, shards(): lax.all_to_all(both.reshape(XY, 4 * MID, width), ('x', 'y'), split_axis=0...  5.52 us
  transfers between devices with their start and end apart: 4, of which 4 were waited for; matrix products, arithmetic and copies ran while one was open for 3% of the time, Pallas kernels for 13%

profile of v1, /device:TPU:1, one launch (start us, length us, event | category | flops | bytes accessed | tf_op | source)
XLA Modules:
  0.0 101.2 jit_solution(1718092062482792677)
XLA Ops:
  0.6 7.6 %all-to-all-start = ((f32[16,64,128]{2,1,0:T(8,128)}), f32[16,64,128]{2,1,0:T(8,128)S(1)}, u32[]{:S(2)}, u32[]{:S(2)}) async-start(f32[16,64,128]{2,1,0:T(8,128)} %bitcast.29), calls=%async_computation | async-start | bytes 1048576 | tf_op jit(solution)/shard_map/all_to_all | solution.py:259
  8.2 0.9 copy.12
  9.2 1.1 %pad_maximum_fusion = f32[16,2,32,32]{3,2,0,1:T(8,128)S(1)} fusion(f32[6,2,32,32]{3,2,0,1:T(8,128)S(1)} %bitcast.27, f32[4,2,32,32]{3,2,1,0:T(8,128)} %param.11, f32[3,2,32,32]{3,2,1,0:T(8,128)} %param.12, f32[3,2,32,32]{3,2,1,0:T(8,128)} %param.15), kind=kLoop, calls=%fused_computation | loop fusion | flops 98304 | bytes 262144 | tf_op jit(solution)/shard_map/concatenate | solution.py:263
  10.3 0.1 pad_add_fusion.where_ref
  10.4 0.2 maximum_maximum_fusion.small_ref
  10.6 1.4 %prep_top.1.top_ref = bf16[2,2,128,256]{3,2,1,0:T(8,128)(2,1)S(1)} custom-call(f32[16,64,64]{2,1,0:T(8,128)S(1)} %maximum_maximum_fusion.small_ref, s32[3]{0:T(128)S(1)} %pad_add_fusion.where_ref), custom_call_target="tpu_custom_call" | custom-call | tf_op jit(solution)/shard_map/prep_top/pallas_call | solution.py:271
  12.0 6.6 %all-to-all-done = f32[16,64,128]{2,1,0:T(8,128)S(1)} async-done(((f32[16,64,128]{2,1,0:T(8,128)}), f32[16,64,128]{2,1,0:T(8,128)S(1)}, u32[]{:S(2)}, u32[]{:S(2)}) %all-to-all-start) | async-done | bytes 524320 | tf_op jit(solution)/shard_map/all_to_all | solution.py:259
  18.6 0.7 top.1
  19.2 7.0 %collective-permute-start = (f32[16,2,32,128]{3,2,1,0:T(8,128)S(1)}, f32[16,2,32,128]{3,2,1,0:T(8,128)S(1)}, u32[]{:S(2)}, u32[]{:S(2)}) collective-permute-start(f32[16,2,32,128]{3,2,1,0:T(8,128)S(1)} %get-tuple-element.10), channel_id=1, source_target_pairs={{0,8},{8,0},{1,9},{9,1},{2,10},{10,2},{3,11},{11,3},{4,12},{12,4},... | collective-permute-start | bytes 1572872 | tf_op jit(solution)/shard_map/ppermute | solution.py:281
  26.2 12.3 %collective-permute-done.got_ref = f32[16,2,32,128]{3,2,1,0:T(8,128)S(1)} collective-permute-done((f32[16,2,32,128]{3,2,1,0:T(8,128)S(1)}, f32[16,2,32,128]{3,2,1,0:T(8,128)S(1)}, u32[]{:S(2)}, u32[]{:S(2)}) %collective-permute-start) | collective-permute-done | bytes 524320 | tf_op jit(solution)/shard_map/ppermute | solution.py:281
  38.5 1.0 %add.25 = f32[16,2,2,32,128]{4,3,2,1,0:T(8,128)} custom-call(f32[16,2,32,128]{3,2,1,0:T(8,128)S(1)} %get-tuple-element.9.own_ref, f32[16,2,32,128]{3,2,1,0:T(8,128)S(1)} %collective-permute-done.got_ref), custom_call_target="tpu_custom_call" | custom-call | tf_op jit(solution)/shard_map/add/pallas_call | solution.py:282
  39.6 0.0 copy-start.4
  39.6 0.0 copy-start.5
  39.6 0.0 copy-start.6
  39.6 0.0 copy-start.7
  39.6 0.0 copy-start.8
  39.6 3.9 %all-to-all-start.1 = ((f32[16,128,128]{2,1,0:T(8,128)}), f32[16,128,128]{2,1,0:T(8,128)S(1)}, u32[]{:S(2)}, u32[]{:S(2)}) async-start(f32[16,128,128]{2,1,0:T(8,128)} %bitcast.7), calls=%async_computation.1 | async-start | bytes 2097152 | tf_op jit(solution)/shard_map/all_to_all | solution.py:283
  43.5 0.0 copy-done.4
  43.5 0.1 copy.16
  43.7 0.0 copy-done.5
  43.7 0.1 copy.17
  43.8 0.0 copy-done.6
  43.8 0.0 copy-done.7
  43.8 0.0 copy-done.8
  43.8 0.1 pad_add_fusion.1.masks_ref
  44.0 0.2 maximum_maximum_fusion.1.large_ref
  44.1 6.7 %prep_blocks.1 = (bf16[3,2,256,512]{3,2,1,0:T(8,128)(2,1)S(1)}, bf16[4,2,128,256]{3,2,1,0:T(8,128)(2,1)S(1)}, bf16[4,2,128,256]{3,2,1,0:T(8,128)(2,1)S(1)}) custom-call(f32[16,64,64]{2,1,0:T(8,128)S(1)} %maximum_maximum_fusion.small_ref, f32[6,128,128]{2,1,0:T(8,128)S(1)} %maximum_maximum_fusion.1.large_ref, s32[9]{0:T(128)S(1)} %pad_add_fusion.1.masks_ref, ...), custom_call_target="tpu_custom_call" | custom-call | tf_op jit(solution)/shard_map/prep_blocks/pallas_call | solution.py:272
  50.8 0.0 copy-start
  50.8 0.8 copy-done
  51.6 0.0 copy-start.2
  51.6 0.8 copy-done.2
  52.4 5.5 %all-to-all-done.1 = f32[16,128,128]{2,1,0:T(8,128)S(1)} async-done(((f32[16,128,128]{2,1,0:T(8,128)}), f32[16,128,128]{2,1,0:T(8,128)S(1)}, u32[]{:S(2)}, u32[]{:S(2)}) %all-to-all-start.1) | async-done | bytes 1048608 | tf_op jit(solution)/shard_map/all_to_all | solution.py:283
  57.9 0.0 copy-start.1
  57.9 1.0 %copy-done.1 = bf16[4,2,128,256]{3,2,1,0:T(8,128)(2,1)S(1)} copy-done((bf16[4,2,128,256]{3,2,1,0:T(8,128)(2,1)S(1)}, bf16[4,2,128,256]{3,2,1,0:T(8,128)(2,1)}, u32[]{:S(2)}) %copy-start.1) | copy-done | bytes 524312
  59.0 0.0 copy-start.3
  59.0 1.0 %copy-done.3 = bf16[4,2,128,256]{3,2,1,0:T(8,128)(2,1)S(1)} copy-done((bf16[4,2,128,256]{3,2,1,0:T(8,128)(2,1)S(1)}, bf16[4,2,128,256]{3,2,1,0:T(8,128)(2,1)}, u32[]{:S(2)}) %copy-start.3) | copy-done | bytes 524312
  60.0 4.4 %send.1 = f32[32,32,128]{2,1,0:T(8,128)S(1)} custom-call(f32[16,2,2,32,128]{4,3,2,1,0:T(8,128)S(1)} %bitcast.24, bf16[3,2,256,512]{3,2,1,0:T(8,128)(2,1)S(1)} %get-tuple-element.11.high_ref, bf16[4,2,128,256]{3,2,1,0:T(8,128)(2,1)S(1)} %copy-done.1, bf16[4,2,128,256]{3,2,1,0:T(8,128)(2,1)S(1)} %copy-done.3), custom_call_target="tpu_custom_call" | custom-call | tf_op jit(solution)/shard_map/send/pallas_call | solution.py:287
  64.5 13.3 %collective-permute-start.1 = (f32[32,32,128]{2,1,0:T(8,128)S(1)}, f32[32,32,128]{2,1,0:T(8,128)S(1)}, u32[]{:S(2)}, u32[]{:S(2)}) collective-permute-start(f32[32,32,128]{2,1,0:T(8,128)S(1)} %send.1), channel_id=1, source_target_pairs={{0,4},{1,5},{2,6},{3,7},{4,0},{5,1},{6,2},{7,3},{8,12},{9,13},{10,... | collective-permute-start | bytes 1572872 | tf_op jit(solution)/shard_map/ppermute | solution.py:288
  77.7 5.0 %keep.1 = (f32[32,32,128]{2,1,0:T(8,128)}, f32[32,32,128]{2,1,0:T(8,128)S(1)}) custom-call(f32[16,2,2,32,128]{4,3,2,1,0:T(8,128)S(1)} %bitcast.25, bf16[3,2,256,512]{3,2,1,0:T(8,128)(2,1)S(1)} %get-tuple-element.11.high_ref, bf16[4,2,128,256]{3,2,1,0:T(8,128)(2,1)S(1)} %copy-done.1, bf16[4,2,128,256]{3,2,1,0:T(8,128)(2,1)S(1)} %copy-done.3), custom_call_target="tpu_custom_call" | custom-call | tf_op jit(solution)/shard_map/keep/pallas_call | solution.py:289
  82.7 17.6 %collective-permute-done.1 = f32[32,32,128]{2,1,0:T(8,128)S(1)} collective-permute-done((f32[32,32,128]{2,1,0:T(8,128)S(1)}, f32[32,32,128]{2,1,0:T(8,128)S(1)}, u32[]{:S(2)}, u32[]{:S(2)}) %collective-permute-start.1) | collective-permute-done | bytes 524320 | tf_op jit(solution)/shard_map/ppermute | solution.py:288
  100.3 0.9 add.16
  (4 shorter events, 0.1 us)
Async XLA Ops:
  0.6 18.0 %all-to-all-start = ((f32[16,64,128]{2,1,0:T(8,128)}), f32[16,64,128]{2,1,0:T(8,128)S(1)}, u32[]{:S(2)}, u32[]{:S(2)}) async-start(f32[16,64,128]{2,1,0:T(8,128)} %bitcast.29), calls=%async_computation | async-start | bytes 1048576 | tf_op jit(solution)/shard_map/all_to_all | solution.py:259
  19.2 19.3 %collective-permute-start = (f32[16,2,32,128]{3,2,1,0:T(8,128)S(1)}, f32[16,2,32,128]{3,2,1,0:T(8,128)S(1)}, u32[]{:S(2)}, u32[]{:S(2)}) collective-permute-start(f32[16,2,32,128]{3,2,1,0:T(8,128)S(1)} %get-tuple-element.10), channel_id=1, source_target_pairs={{0,8},{8,0},{1,9},{9,1},{2,10},{10,2},{3,11},{11,3},{4,12},{12,4},... | collective-permute-start | bytes 1572872 | tf_op jit(solution)/shard_map/ppermute | solution.py:281
  39.6 3.9 %copy-start.4 = (f32[3,2,64,64]{3,2,1,0:T(8,128)S(1)}, f32[3,2,64,64]{3,2,1,0:T(8,128)}, u32[]{:S(2)}) copy-start(f32[3,2,64,64]{3,2,1,0:T(8,128)} %param.13) | copy-start | bytes 294916
  39.6 4.1 %copy-start.5 = (f32[3,2,64,64]{3,2,1,0:T(8,128)S(1)}, f32[3,2,64,64]{3,2,1,0:T(8,128)}, u32[]{:S(2)}) copy-start(f32[3,2,64,64]{3,2,1,0:T(8,128)} %param.16) | copy-start | bytes 294916
  39.6 4.2 %copy-start.6 = (s32[3]{0:T(128)S(1)}, s32[3]{0:T(128)}, u32[]{:S(2)}) copy-start(s32[3]{0:T(128)} %param.19) | copy-start | bytes 40
  39.6 4.2 %copy-start.7 = (s32[3]{0:T(128)S(1)}, s32[3]{0:T(128)}, u32[]{:S(2)}) copy-start(s32[3]{0:T(128)} %param.18) | copy-start | bytes 40
  39.6 4.2 %copy-start.8 = (s32[3]{0:T(128)S(1)}, s32[3]{0:T(128)}, u32[]{:S(2)}) copy-start(s32[3]{0:T(128)} %param.17) | copy-start | bytes 40
  39.6 18.3 %all-to-all-start.1 = ((f32[16,128,128]{2,1,0:T(8,128)}), f32[16,128,128]{2,1,0:T(8,128)S(1)}, u32[]{:S(2)}, u32[]{:S(2)}) async-start(f32[16,128,128]{2,1,0:T(8,128)} %bitcast.7), calls=%async_computation.1 | async-start | bytes 2097152 | tf_op jit(solution)/shard_map/all_to_all | solution.py:283
  50.8 0.8 copy-start
  51.6 0.8 copy-start.2
  57.9 1.0 %copy-start.1 = (bf16[4,2,128,256]{3,2,1,0:T(8,128)(2,1)S(1)}, bf16[4,2,128,256]{3,2,1,0:T(8,128)(2,1)}, u32[]{:S(2)}) copy-start(bf16[4,2,128,256]{3,2,1,0:T(8,128)(2,1)} %copy-done) | copy-start | bytes 1572868
  59.0 1.0 %copy-start.3 = (bf16[4,2,128,256]{3,2,1,0:T(8,128)(2,1)S(1)}, bf16[4,2,128,256]{3,2,1,0:T(8,128)(2,1)}, u32[]{:S(2)}) copy-start(bf16[4,2,128,256]{3,2,1,0:T(8,128)(2,1)} %copy-done.2) | copy-start | bytes 1572868
  64.5 35.9 %collective-permute-start.1 = (f32[32,32,128]{2,1,0:T(8,128)S(1)}, f32[32,32,128]{2,1,0:T(8,128)S(1)}, u32[]{:S(2)}, u32[]{:S(2)}) collective-permute-start(f32[32,32,128]{2,1,0:T(8,128)S(1)} %send.1), channel_id=1, source_target_pairs={{0,4},{1,5},{2,6},{3,7},{4,0},{5,1},{6,2},{7,3},{8,12},{9,13},{10,... | collective-permute-start | bytes 1572872 | tf_op jit(solution)/shard_map/ppermute | solution.py:288

commit v2 on v1

v2 whole, which is shorter than its diff:
```python
import jax
import jax.numpy as jnp
from jax import lax
from jax.experimental import pallas as pl
from jax.experimental.pallas import tpu as pltpu
from jax.sharding import Mesh, PartitionSpec as P


TOP = 32
MID = 32
LOW = 64
BLOCKS = 3
XY = 16
EARLY = 8
HIGH = lax.Precision.HIGHEST
F32 = jnp.float32
BF16 = jnp.bfloat16


def split(value):
    high = value.astype(BF16)
    return high, (value - high.astype(F32)).astype(BF16)


def dot3(left, right):
    high, low = left
    upper, lower = right
    return jnp.dot(
        jnp.concatenate([high, low, high], axis=1),
        jnp.concatenate([upper, upper, lower], axis=0),
        preferred_element_type=F32,
    )


def times_i(value):
    lane = lax.broadcasted_iota(jnp.int32, value.shape, 1)
    turned = pltpu.roll(value, LOW, 1)
    return jnp.where(lane < LOW, -turned, turned)


def iotas(shape):
    return lax.broadcasted_iota(jnp.int32, shape, 0), lax.broadcasted_iota(jnp.int32, shape, 1)


def sign_of(bits):
    for offset in (8, 4, 2, 1):
        bits = jnp.bitwise_xor(bits, jnp.right_shift(bits, offset))
    return (1 - 2 * jnp.bitwise_and(bits, 1)).astype(F32)


def hdot(left, right):
    return jnp.dot(left, right, precision=HIGH, preferred_element_type=F32)


def fold_left(order, flip, phase):
    row, col = iotas((order, order))
    return jnp.where(col == jnp.bitwise_xor(row, flip), sign_of(jnp.bitwise_and(col, phase)), 0.0)


def fold_right(order, flip, phase):
    row, col = iotas((order, order))
    return jnp.where(row == jnp.bitwise_xor(col, flip), sign_of(jnp.bitwise_and(row, phase)), 0.0)


def put(ref, index, value):
    high, low = split(value)
    ref[index, 0] = high
    ref[index, 1] = low


def prep_top(small_ref, where_ref, top_ref):
    zh = where_ref[1]
    total = hdot(hdot(small_ref[3], small_ref[2]), hdot(small_ref[1], small_ref[0]))
    row, col = iotas((TOP, 8 * XY))
    in_pick = jnp.where(row == 2 * (col // 8) + zh, 1.0, 0.0)
    wide = hdot(total[:, :TOP], in_pick)
    row, col = iotas((8 * XY, 8 * XY))
    same = jnp.where(row % 8 == col % 8, 1.0, 0.0)
    row, col = iotas((8 * XY, TOP))
    for index in range(2):
        pick = jnp.where(col == 2 * (row // 8) + (zh if index == 0 else 1 - zh), 1.0, 0.0)
        put(
            top_ref,
            index,
            jnp.concatenate([hdot(pick, wide[:TOP]) * same, hdot(pick, wide[TOP:]) * same], axis=1),
        )


def spread_high(matrix, scale):
    row, col = iotas((TOP, 8 * TOP))
    wide = hdot(matrix[:, :TOP], jnp.where(row == col // 8, 1.0, 0.0))
    row, col = iotas((8 * TOP, TOP))
    pick = jnp.where(col == row // 8, 1.0, 0.0)
    row, col = iotas((8 * TOP, 8 * TOP))
    same = jnp.where(row % 8 == col % 8, scale, 0.0)
    return jnp.concatenate([hdot(pick, wide[:TOP]) * same, hdot(pick, wide[TOP:]) * same], axis=0)


def spread_mid(matrix):
    row, col = iotas((MID, 4 * MID))
    wide = hdot(matrix[:, :MID], jnp.where(row == col % MID, 1.0, 0.0))
    row, col = iotas((4 * MID, MID))
    pick = jnp.where(col == row % MID, 1.0, 0.0)
    row, col = iotas((4 * MID, 4 * MID))
    same = jnp.where(row // MID == col // MID, 1.0, 0.0)
    return jnp.concatenate([hdot(pick, wide[:MID]) * same, hdot(pick, wide[MID:]) * same], axis=1)


def prep_block(refs, block, slot, mid, low):
    small_ref, large_ref, masks_ref, where_ref, high_ref, mid_ref, low_ref = refs
    flip, phase = masks_ref[block], masks_ref[BLOCKS + block]
    source = where_ref[0] if block == 1 else jnp.bitwise_xor(where_ref[0], where_ref[2])
    scale = sign_of(jnp.bitwise_and(source, masks_ref[2 * BLOCKS + block]))
    fold = fold_left(2 * TOP, flip // (MID * LOW), phase // (MID * LOW))
    high = hdot(fold, hdot(small_ref[8 + 2 * block], small_ref[7 + 2 * block]))
    put(high_ref, slot, spread_high(high, scale))
    fold = fold_left(2 * MID, flip // LOW % MID, phase // LOW % MID)
    put(mid_ref, slot, spread_mid(hdot(fold, hdot(small_ref[13 + block], mid))))
    fold = fold_right(2 * LOW, flip % LOW, phase % LOW)
    full = hdot(hdot(low, large_ref[3 + block]), fold)
    put(low_ref, slot, jnp.concatenate([full, times_i(full)], axis=1))


def merged(small_ref, large_ref):
    mid = hdot(hdot(small_ref[6], small_ref[5]), small_ref[4])
    return mid, hdot(hdot(large_ref[0], large_ref[1]), large_ref[2])


def prep_send(small_ref, large_ref, masks_ref, where_ref, high_ref, mid_ref, low_ref, built_ref, sems):
    mid, low = merged(small_ref, large_ref)
    refs = (small_ref, large_ref, masks_ref, where_ref, built_ref, mid_ref, low_ref)
    copies = [pltpu.make_async_copy(built_ref.at[slot], high_ref.at[slot], sems.at[slot]) for slot in range(2)]
    for slot in range(2):
        prep_block(refs, slot + 1, slot, mid, low)
        copies[slot].start()
    for copy in copies:
        copy.wait()


def prep_keep(*refs):
    mid, low = merged(*refs[:2])
    prep_block(refs, 0, 0, mid, low)
    put(refs[5], 1, spread_mid(mid))
    put(refs[6], 1, jnp.concatenate([low, times_i(low)], axis=1))


def two_streams(out_ref, first, value):
    half = XY // 2
    out_ref[:, first] = value
    out_ref[:half, first + 1] = value[half:]
    out_ref[half:, first + 1] = value[:half]


def top_kernel(field_ref, top_ref, own_ref, other_ref, early_ref):
    for rest in range(2):
        for pair in range(2):
            parts = [
                field_ref[:, rest, 16 * pair + 8 * half : 16 * pair + 8 * half + 8, :].reshape(8 * XY, 2 * LOW)
                for half in range(2)
            ]
            right = jnp.concatenate(
                [jnp.concatenate(parts, axis=1), jnp.concatenate([times_i(part) for part in parts], axis=1)], axis=0
            )
            right = split(right)
            for index, out_ref in enumerate((own_ref, other_ref)):
                done = dot3((top_ref[index, 0], top_ref[index, 1]), right)
                for half in range(2):
                    group = 2 * pair + half
                    value = done[:, 2 * LOW * half : 2 * LOW * (half + 1)].reshape(XY, 8, 2 * LOW)
                    if group == 0:
                        two_streams(early_ref.at[:, :, rest], 2 * index, value)
                    else:
                        out_ref[:, rest, 8 * group - EARLY : 8 * group - EARLY + 8, :] = value


def add_kernel(own_ref, got_ref, out_ref):
    two_streams(out_ref, 0, own_ref[...] + got_ref[...])


def low_mid(load, mid, low, store):
    for group in range(4):
        done = dot3(split(load(group)), low)
        same, turned = done[:, : 2 * LOW], done[:, 2 * LOW :]
        right = jnp.concatenate(
            [
                jnp.concatenate([same[: 4 * MID], same[4 * MID :]], axis=1),
                jnp.concatenate([turned[: 4 * MID], turned[4 * MID :]], axis=1),
            ],
            axis=0,
        )
        done = dot3(mid, split(right))
        store(group, jnp.concatenate([done[:, : 2 * LOW], done[:, 2 * LOW :]], axis=0))


def pair_of(ref, index):
    return ref[index, 0], ref[index, 1]


def high_step(sources, matrices, out_ref):
    rows = 8 * TOP
    for pair in range(2):
        total = None
        for source_ref, matrix in zip(sources, matrices):
            parts = [
                source_ref[:, 16 * pair + 8 * half : 16 * pair + 8 * half + 8, :].reshape(rows, 2 * LOW)
                for half in range(2)
            ]
            done = dot3(matrix, split(jnp.concatenate(parts, axis=1)))
            total = done if total is None else total + done
        for half in range(2):
            part = total[:, 2 * LOW * half : 2 * LOW * (half + 1)]
            value = part[:rows] + times_i(part[rows:])
            out_ref[:, 16 * pair + 8 * half : 16 * pair + 8 * half + 8, :] = value.reshape(TOP, 8, 2 * LOW)


def reader(fields, stream):
    early_ref, got_ref, late_ref = fields

    def load(group):
        part = slice(4 * group, 4 * group + 4)
        early = early_ref[part, stream] + got_ref[part, stream]
        return jnp.concatenate(
            [early.reshape(8, EARLY, 2 * LOW), late_ref[part, stream].reshape(8, MID - EARLY, 2 * LOW)], axis=1
        ).reshape(8 * MID, 2 * LOW)

    return load


def writer(ref):
    def store(group, value):
        ref[8 * group : 8 * group + 8] = value.reshape(8, MID, 2 * LOW)

    return store


def send_kernel(early_ref, got_ref, late_ref, high_ref, mid_ref, low_ref, out_ref, first_ref, second_ref, held_ref, sems):
    fields = (early_ref, got_ref, late_ref)
    copies = [pltpu.make_async_copy(high_ref.at[slot], held_ref.at[slot], sems.at[slot]) for slot in range(2)]
    for copy in copies:
        copy.start()
    low_mid(reader(fields, 0), pair_of(mid_ref, 0), pair_of(low_ref, 0), writer(first_ref))
    low_mid(reader(fields, 1), pair_of(mid_ref, 1), pair_of(low_ref, 1), writer(second_ref))
    for copy in copies:
        copy.wait()
    high_step((first_ref, second_ref), (pair_of(held_ref, 0), pair_of(held_ref, 1)), out_ref)


def keep_kernel(early_ref, got_ref, late_ref, high_ref, mid_ref, low_ref, final_ref, out_ref, first_ref):
    fields = (early_ref, got_ref, late_ref)
    low_mid(reader(fields, 1), pair_of(mid_ref, 0), pair_of(low_ref, 0), writer(first_ref))
    high_step((first_ref,), (pair_of(high_ref, 0),), out_ref)
    low_mid(reader(fields, 0), pair_of(mid_ref, 1), pair_of(low_ref, 1), writer(final_ref))


def real_form(matrix):
    real, imag = matrix[:, 0], matrix[:, 1]
    return jnp.concatenate(
        [jnp.concatenate([real, -imag], axis=2), jnp.concatenate([imag, real], axis=2)], axis=1
    )


def flat_form(matrix):
    real, imag = jnp.swapaxes(matrix[:, 0], 1, 2), jnp.swapaxes(matrix[:, 1], 1, 2)
    return jnp.concatenate(
        [jnp.concatenate([real, imag], axis=2), jnp.concatenate([-imag, real], axis=2)], axis=1
    )


def vm():
    return pl.BlockSpec(memory_space=pltpu.VMEM)


def sm():
    return pl.BlockSpec(memory_space=pltpu.SMEM)


def call(body, ins, outs, scratch=(), smem=(), far_in=(), far_out=(), copies=0):
    far = pl.BlockSpec(memory_space=pltpu.HBM)
    held = [pltpu.VMEM(s, t) for s, t in scratch]
    if copies:
        held.append(pltpu.SemaphoreType.DMA((copies,)))
    return pl.pallas_call(
        body,
        in_specs=[sm() if i in smem else far if i in far_in else vm() for i in range(ins)],
        out_specs=[far if i in far_out else vm() for i in range(len(outs))],
        out_shape=[jax.ShapeDtypeStruct(s, t) for s, t in outs],
        scratch_shapes=held,
        compiler_params=pltpu.CompilerParams(vmem_limit_bytes=16 * 2**20),
    )


def evolve(
    amplitudes,
    top_gates,
    mid_gates,
    low_gates,
    ham_top,
    ham_mid,
    ham_low,
    flip_masks,
    phase_masks,
    device_phase_masks,
):
    width = 2 * LOW
    inside = lax.all_to_all(
        amplitudes.reshape(XY, 2 * MID, width), ("x", "y"), split_axis=0, concat_axis=0, tiled=True
    ).reshape(XY, 2, MID, width)
    small = real_form(
        jnp.concatenate([top_gates, mid_gates, ham_top.reshape(2 * BLOCKS, 2, TOP, TOP), ham_mid], axis=0)
    )
    large = flat_form(jnp.concatenate([low_gates, ham_low], axis=0))
    zh = lax.axis_index("zh")
    n = lax.axis_index("narrow")
    device_id = ((lax.axis_index("x") * 4 + lax.axis_index("y")) * 2 + zh) * 8 + n
    where = jnp.stack([device_id, zh, jnp.int32(16 * 8)]).astype(jnp.int32)
    masks = jnp.concatenate([flip_masks, phase_masks, device_phase_masks])
    (top,) = call(prep_top, 2, [((2, 2, 128, 256), BF16)], smem=(1,))(small, where)
    late = MID - EARLY
    piece = ((XY, 2, late, width), F32)
    own, other, early = call(top_kernel, 2, [piece, piece, ((XY, 4, 2, EARLY, width), F32)])(inside, top)
    swap = [(0, 1), (1, 0)]
    got = lax.ppermute(other, "zh", swap)
    early = lax.all_to_all(
        early.reshape(XY, 8 * EARLY, width), ("x", "y"), split_axis=0, concat_axis=0, tiled=True
    ).reshape(XY, 4, 2, EARLY, width)
    prepared = [((2, 2, 512, 256), BF16), ((2, 2, 128, 256), BF16), ((2, 2, 128, 256), BF16)]
    high, mid, low = call(
        prep_send, 4, prepared, prepared[:1], smem=(2, 3), far_out=(0,), copies=2
    )(small, large, masks, where)
    early_got = lax.ppermute(early[:, 2:], "zh", swap)
    (both,) = call(add_kernel, 2, [((XY, 2, 2, late, width), F32)])(own, got)
    field = lax.all_to_all(
        both.reshape(XY, 4 * late, width), ("x", "y"), split_axis=0, concat_axis=0, tiled=True
    ).reshape(XY, 2, 2, late, width)
    whole = ((TOP, MID, width), F32)
    fields = (early, early_got, field)
    (sent,) = call(
        send_kernel, 6, [whole], [whole, whole] + prepared[:1], far_in=(3,), copies=2
    )(*fields, high, mid, low)
    arrived = lax.ppermute(sent, "narrow", [(i, i ^ 4) for i in range(8)])
    prepared = [((1, 2, 512, 256), BF16)] + prepared[1:]
    high, mid, low = call(prep_keep, 4, prepared, smem=(2, 3))(small, large, masks, where)
    final, kept = call(keep_kernel, 6, [whole, whole], [whole])(*fields, high, mid, low)
    cotangent = kept + arrived
    return final.reshape(TOP * MID, width), cotangent.reshape(TOP * MID, width)


def solution(mesh):
    fine = Mesh(mesh.devices.reshape(4, 4, 2, 8), ("x", "y", "zh", "narrow"))
    rows = P(("x", "y", "zh", "narrow"), None)
    return jax.shard_map(
        evolve,
        mesh=fine,
        in_specs=(rows, P(), P(), P(), P(), P(), P(), P(), P(), P()),
        out_specs=(rows, rows),
        check_vma=False,
    )
```

time: 102 us -> 102 us (level)
  waiting for transfers between devices: 42 us -> 30.4 us
  starting transfers between devices: 31.7 us -> 42.4 us
  Pallas kernels: 19.2 us -> 20.4 us
    ppermute x2 -> x3, waiting for transfers between devices: 29.9 us -> 22.9 us  [the longest x1 14.5 us: evolve(): arrived = lax.ppermute(sent, 'narrow', [(i, i ^ 4) for i in range(8)])]
    all_to_all x2 -> x3, starting transfers between devices: 11.5 us -> 17.6 us  [the longest x1 7.72 us: evolve(): lax.all_to_all(amplitudes.reshape(XY, 2 * MID, width), ('x', 'y'), split_...]
    all_to_all x2 -> x3, waiting for transfers between devices: 12.1 us -> 7.51 us  [the longest x1 7.51 us: evolve(): lax.all_to_all(amplitudes.reshape(XY, 2 * MID, width), ('x', 'y'), split_...]
    ppermute x2 -> x3, starting transfers between devices: 20.2 us -> 24.7 us  [the longest x1 12.5 us: evolve(): arrived = lax.ppermute(sent, 'narrow', [(i, i ^ 4) for i in range(8)])]
    pallas_call x6 -> x7, Pallas kernels: 19.2 us -> 20.4 us  [the longest x1 5.01 us: evolve(): call(prep_send, 4, prepared, prepared[:1], smem=(2, 3), far_out=(0,), cop...]
    unnamed x21 -> x29, local copies, waits for them, and re-layouts: 4.85 us -> 5.33 us
  transfers between devices with their start and end apart: 4 -> 6, of which waited for: 4 -> 3; matrix products, arithmetic and copies ran while one was open for 3% -> 1% of each run, Pallas kernels for 13% -> 15%
where the time goes in v2:
time: 102 us; the launch traced here: 101 us
  starting transfers between devices  42.4 us (42%)
  waiting for transfers between devices  30.4 us (30%)
  Pallas kernels  20.4 us (20%)
  local copies, waits for them, and re-layouts  5.38 us (5%)
  other arithmetic  1.51 us (1%)
    ppermute x1, waiting for transfers between devices, evolve(): arrived = lax.ppermute(sent, 'narrow', [(i, i ^ 4) for i in range(8)])  14.5 us
    ppermute x1, starting transfers between devices, evolve(): arrived = lax.ppermute(sent, 'narrow', [(i, i ^ 4) for i in range(8)])  12.5 us
    ppermute x1, waiting for transfers between devices, evolve(): got = lax.ppermute(other, 'zh', swap)  8.4 us
    all_to_all x1, starting transfers between devices, evolve(): lax.all_to_all(amplitudes.reshape(XY, 2 * MID, width), ('x', 'y'), split_...  7.72 us
    all_to_all x1, waiting for transfers between devices, evolve(): lax.all_to_all(amplitudes.reshape(XY, 2 * MID, width), ('x', 'y'), split_...  7.51 us
    ppermute x1, starting transfers between devices, evolve(): got = lax.ppermute(other, 'zh', swap)  6.99 us
    all_to_all x1, starting transfers between devices, evolve(): lax.all_to_all(both.reshape(XY, 4 * late, width), ('x', 'y'), split_axis=...  6.36 us
    unnamed x29, local copies, waits for them, and re-layouts  5.33 us
  transfers between devices with their start and end apart: 6, of which 3 were waited for; matrix products, arithmetic and copies ran while one was open for 1% of the time, Pallas kernels for 15%

profile of v2, /device:TPU:1, one launch (start us, length us, event | category | flops | bytes accessed | tf_op | source)
XLA Modules:
  0.0 100.9 jit_solution(6697847465070231361)
XLA Ops:
  0.6 0.0 copy-start.4
  0.6 7.7 %all-to-all-start = ((f32[16,64,128]{2,1,0:T(8,128)}), f32[16,64,128]{2,1,0:T(8,128)S(1)}, u32[]{:S(2)}, u32[]{:S(2)}) async-start(f32[16,64,128]{2,1,0:T(8,128)} %bitcast.34), calls=%async_computation | async-start | bytes 1048576 | tf_op jit(solution)/shard_map/all_to_all | solution.py:305
  8.4 0.0 copy-done.4
  8.4 0.0 copy-start.7
  8.4 0.0 copy-start.8
  8.4 0.0 copy-start.9
  8.4 0.8 copy-done.7
  9.3 0.1 copy-done.8
  9.3 0.0 copy-done.9
  9.5 0.1 pad_add_fusion.where_ref.refs_3_
  9.6 0.2 maximum_maximum_fusion.small_ref.refs_0_
  9.8 1.4 %shard_map.113.top_ref = bf16[2,2,128,256]{3,2,1,0:T(8,128)(2,1)S(1)} custom-call(f32[16,64,64]{2,1,0:T(8,128)S(1)} %maximum_maximum_fusion.small_ref.refs_0_, s32[3]{0:T(128)S(1)} %pad_add_fusion.where_ref.refs_3_), custom_call_target="tpu_custom_call" | custom-call | tf_op jit(solution)/shard_map/pallas_call | solution.py:317
  11.2 7.5 %all-to-all-done = f32[16,64,128]{2,1,0:T(8,128)S(1)} async-done(((f32[16,64,128]{2,1,0:T(8,128)}), f32[16,64,128]{2,1,0:T(8,128)S(1)}, u32[]{:S(2)}, u32[]{:S(2)}) %all-to-all-start) | async-done | bytes 524320 | tf_op jit(solution)/shard_map/all_to_all | solution.py:305
  18.7 1.4 %shard_map.114 = (f32[16,2,24,128]{3,2,1,0:T(8,128)S(1)}, f32[16,2,24,128]{3,2,1,0:T(8,128)S(1)}, f32[16,4,2,8,128]{4,3,2,1,0:T(8,128)}) custom-call(f32[16,2,32,128]{3,2,1,0:T(8,128)S(1)} %bitcast.31, bf16[2,2,128,256]{3,2,1,0:T(8,128)(2,1)S(1)} %shard_map.113.top_ref), custom_call_target="tpu_custom_call" | custom-call | tf_op jit(solution)/shard_map/pallas_call | solution.py:320
  20.1 3.6 %all-to-all-start.1 = ((f32[16,64,128]{2,1,0:T(8,128)}), f32[16,64,128]{2,1,0:T(8,128)S(1)}, u32[]{:S(2)}, u32[]{:S(2)}) async-start(f32[16,64,128]{2,1,0:T(8,128)} %bitcast.7), calls=%async_computation.1 | async-start | bytes 1048576 | tf_op jit(solution)/shard_map/all_to_all | solution.py:323
  23.7 7.0 %collective-permute-start.1 = (f32[16,2,24,128]{3,2,1,0:T(8,128)S(1)}, f32[16,2,24,128]{3,2,1,0:T(8,128)S(1)}, u32[]{:S(2)}, u32[]{:S(2)}) collective-permute-start(f32[16,2,24,128]{3,2,1,0:T(8,128)S(1)} %get-tuple-element.15), channel_id=1, source_target_pairs={{0,8},{8,0},{1,9},{9,1},{2,10},{10,2},{3,11},{11,3},{4,12},{12,4},... | collective-permute-start | bytes 1179656 | tf_op jit(solution)/shard_map/ppermute | solution.py:322
  30.7 8.4 %collective-permute-done.1.got_ref = f32[16,2,24,128]{3,2,1,0:T(8,128)S(1)} collective-permute-done((f32[16,2,24,128]{3,2,1,0:T(8,128)S(1)}, f32[16,2,24,128]{3,2,1,0:T(8,128)S(1)}, u32[]{:S(2)}, u32[]{:S(2)}) %collective-permute-start.1) | collective-permute-done | bytes 393248 | tf_op jit(solution)/shard_map/ppermute | solution.py:322
  39.1 0.9 shard_map.115
  40.0 0.0 all-to-all-done.1
  40.0 0.0 copy-start.5
  40.0 6.4 %all-to-all-start.2 = ((f32[16,96,128]{2,1,0:T(8,128)}), f32[16,96,128]{2,1,0:T(8,128)S(1)}, u32[]{:S(2)}, u32[]{:S(2)}) async-start(f32[16,96,128]{2,1,0:T(8,128)} %bitcast.9), calls=%async_computation.2 | async-start | bytes 1572864 | tf_op jit(solution)/shard_map/all_to_all | solution.py:332
  46.4 0.0 copy-done.5
  46.4 0.0 copy-start.6
  46.4 0.1 copy.16
  46.5 0.8 copy-done.6
  47.3 0.1 copy.17
  47.4 0.0 copy-start.10
  47.5 0.0 copy-start.11
  47.5 0.0 copy-start.12
  47.5 5.2 %collective-permute-start = (f32[16,2,2,8,128]{4,3,2,1,0:T(8,128)S(1)}, f32[16,2,2,8,128]{4,3,2,1,0:T(8,128)S(1)}, u32[]{:S(2)}, u32[]{:S(2)}) collective-permute-start(f32[16,2,2,8,128]{4,3,2,1,0:T(8,128)S(1)} %slice.22), channel_id=1, source_target_pairs={{0,8},{8,0},{1,9},{9,1},{2,10},{10,2},{3,11},{11,3},{4,12},{12,4},... | collective-permute-start | bytes 786440 | tf_op jit(solution)/shard_map/ppermute | solution.py:330
  52.7 0.0 copy-done.10
  52.7 0.0 copy-done.11
  52.7 0.0 copy-done.12
  52.7 0.1 pad_add_fusion.1.refs_2_.masks_ref
  52.9 0.2 maximum_maximum_fusion.1.refs_1_.large_ref
  53.0 5.0 %shard_map.118 = (bf16[2,2,512,256]{3,2,1,0:T(8,128)(2,1)S(1)}, bf16[2,2,128,256]{3,2,1,0:T(8,128)(2,1)S(1)}, bf16[2,2,128,256]{3,2,1,0:T(8,128)(2,1)S(1)}) custom-call(f32[16,64,64]{2,1,0:T(8,128)S(1)} %maximum_maximum_fusion.small_ref.refs_0_, f32[6,128,128]{2,1,0:T(8,128)S(1)} %maximum_maximum_fusion.1.refs_1_.large_ref, ...), custom_call_target="tpu_custom_call" | custom-call | tf_op jit(solution)/shard_map/pallas_call | solution.py:327
  58.0 0.0 copy-start
  58.1 0.7 copy-done
  58.8 0.0 copy-start.2
  58.8 0.7 copy-done.2
  59.5 0.0 collective-permute-done.got_ref
  59.5 0.0 all-to-all-done.2
  59.5 0.0 copy-start.1
  59.5 0.9 copy-done.1
  60.4 0.0 copy-start.3
  60.4 0.9 copy-done.3
  61.4 4.3 %shard_map.119 = f32[32,32,128]{2,1,0:T(8,128)S(1)} custom-call(f32[16,4,2,8,128]{4,3,2,1,0:T(8,128)S(1)} %bitcast.29, f32[16,2,2,8,128]{4,3,2,1,0:T(8,128)S(1)} %collective-permute-done.got_ref, f32[16,2,2,24,128]{4,3,2,1,0:T(8,128)S(1)} %bitcast.26, bf16[2,2,512,256]{3,2,1,0:T(8,128)(2,1)S(1)} %get-tuple-element.21.high_ref, ...), custom_call_target="tpu_custom_call" | custom-call | tf_op jit(solution)/shard_map/pallas_call | solution.py:337
  65.7 12.5 %collective-permute-start.2 = (f32[32,32,128]{2,1,0:T(8,128)S(1)}, f32[32,32,128]{2,1,0:T(8,128)S(1)}, u32[]{:S(2)}, u32[]{:S(2)}) collective-permute-start(f32[32,32,128]{2,1,0:T(8,128)S(1)} %shard_map.119), channel_id=1, source_target_pairs={{0,4},{1,5},{2,6},{3,7},{4,0},{5,1},{6,2},{7,3},{8,12},{9,13},{10,... | collective-permute-start | bytes 1572872 | tf_op jit(solution)/shard_map/ppermute | solution.py:340
  78.2 2.9 %shard_map.116 = (bf16[1,2,512,256]{3,2,1,0:T(8,128)(2,1)S(1)}, bf16[2,2,128,256]{3,2,1,0:T(8,128)(2,1)S(1)}, bf16[2,2,128,256]{3,2,1,0:T(8,128)(2,1)S(1)}) custom-call(f32[16,64,64]{2,1,0:T(8,128)S(1)} %maximum_maximum_fusion.small_ref.refs_0_, f32[6,128,128]{2,1,0:T(8,128)S(1)} %maximum_maximum_fusion.1.refs_1_.large_ref, ...), custom_call_target="tpu_custom_call" | custom-call | tf_op jit(solution)/shard_map/pallas_call | solution.py:342
  81.1 4.5 %shard_map.117 = (f32[32,32,128]{2,1,0:T(8,128)}, f32[32,32,128]{2,1,0:T(8,128)S(1)}) custom-call(f32[16,4,2,8,128]{4,3,2,1,0:T(8,128)S(1)} %bitcast.30, f32[16,2,2,8,128]{4,3,2,1,0:T(8,128)S(1)} %collective-permute-done.got_ref, f32[16,2,2,24,128]{4,3,2,1,0:T(8,128)S(1)} %bitcast.27, bf16[1,2,512,256]{3,2,1,0:T(8,128)(2,1)S(1)} %get-tuple-element.16.high_ref, ...), custom_call_target="tpu_custom_call" | custom-call | tf_op jit(solution)/shard_map/pallas_call | solution.py:343
  85.5 14.5 %collective-permute-done.2 = f32[32,32,128]{2,1,0:T(8,128)S(1)} collective-permute-done((f32[32,32,128]{2,1,0:T(8,128)S(1)}, f32[32,32,128]{2,1,0:T(8,128)S(1)}, u32[]{:S(2)}, u32[]{:S(2)}) %collective-permute-start.2) | collective-permute-done | bytes 524320 | tf_op jit(solution)/shard_map/ppermute | solution.py:340
  100.0 0.9 add.15
  (7 shorter events, 0.2 us)
Async XLA Ops:
  0.6 7.7 %copy-start.4 = (f32[3,2,2,32,32]{4,3,2,1,0:T(8,128)S(1)}, f32[3,2,2,32,32]{4,3,2,1,0:T(8,128)}, u32[]{:S(2)}) copy-start(f32[3,2,2,32,32]{4,3,2,1,0:T(8,128)} %param.14) | copy-start | bytes 147460
  0.6 18.1 %all-to-all-start = ((f32[16,64,128]{2,1,0:T(8,128)}), f32[16,64,128]{2,1,0:T(8,128)S(1)}, u32[]{:S(2)}, u32[]{:S(2)}) async-start(f32[16,64,128]{2,1,0:T(8,128)} %bitcast.34), calls=%async_computation | async-start | bytes 1048576 | tf_op jit(solution)/shard_map/all_to_all | solution.py:305
  8.4 0.9 copy-start.7
  8.4 0.9 copy-start.8
  8.4 1.0 copy-start.9
  20.1 19.9 %all-to-all-start.1 = ((f32[16,64,128]{2,1,0:T(8,128)}), f32[16,64,128]{2,1,0:T(8,128)S(1)}, u32[]{:S(2)}, u32[]{:S(2)}) async-start(f32[16,64,128]{2,1,0:T(8,128)} %bitcast.7), calls=%async_computation.1 | async-start | bytes 1048576 | tf_op jit(solution)/shard_map/all_to_all | solution.py:323
  23.7 15.4 %collective-permute-start.1 = (f32[16,2,24,128]{3,2,1,0:T(8,128)S(1)}, f32[16,2,24,128]{3,2,1,0:T(8,128)S(1)}, u32[]{:S(2)}, u32[]{:S(2)}) collective-permute-start(f32[16,2,24,128]{3,2,1,0:T(8,128)S(1)} %get-tuple-element.15), channel_id=1, source_target_pairs={{0,8},{8,0},{1,9},{9,1},{2,10},{10,2},{3,11},{11,3},{4,12},{12,4},... | collective-permute-start | bytes 1179656 | tf_op jit(solution)/shard_map/ppermute | solution.py:322
  40.0 6.4 %copy-start.5 = (f32[3,2,64,64]{3,2,1,0:T(8,128)S(1)}, f32[3,2,64,64]{3,2,1,0:T(8,128)}, u32[]{:S(2)}) copy-start(f32[3,2,64,64]{3,2,1,0:T(8,128)} %param.13) | copy-start | bytes 294916
  40.0 19.5 %all-to-all-start.2 = ((f32[16,96,128]{2,1,0:T(8,128)}), f32[16,96,128]{2,1,0:T(8,128)S(1)}, u32[]{:S(2)}, u32[]{:S(2)}) async-start(f32[16,96,128]{2,1,0:T(8,128)} %bitcast.9), calls=%async_computation.2 | async-start | bytes 1572864 | tf_op jit(solution)/shard_map/all_to_all | solution.py:332
  46.4 0.9 copy-start.6
  47.4 5.3 %copy-start.10 = (s32[3]{0:T(128)S(1)}, s32[3]{0:T(128)}, u32[]{:S(2)}) copy-start(s32[3]{0:T(128)} %param.19) | copy-start | bytes 40
  47.5 5.3 %copy-start.11 = (s32[3]{0:T(128)S(1)}, s32[3]{0:T(128)}, u32[]{:S(2)}) copy-start(s32[3]{0:T(128)} %param.18) | copy-start | bytes 40
  47.5 5.3 %copy-start.12 = (s32[3]{0:T(128)S(1)}, s32[3]{0:T(128)}, u32[]{:S(2)}) copy-start(s32[3]{0:T(128)} %param.17) | copy-start | bytes 40
  47.5 11.9 %collective-permute-start = (f32[16,2,2,8,128]{4,3,2,1,0:T(8,128)S(1)}, f32[16,2,2,8,128]{4,3,2,1,0:T(8,128)S(1)}, u32[]{:S(2)}, u32[]{:S(2)}) collective-permute-start(f32[16,2,2,8,128]{4,3,2,1,0:T(8,128)S(1)} %slice.22), channel_id=1, source_target_pairs={{0,8},{8,0},{1,9},{9,1},{2,10},{10,2},{3,11},{11,3},{4,12},{12,4},... | collective-permute-start | bytes 786440 | tf_op jit(solution)/shard_map/ppermute | solution.py:330
  58.0 0.7 copy-start
  58.8 0.7 copy-start.2
  59.5 1.0 copy-start.1
  60.4 0.9 copy-start.3
  65.7 34.3 %collective-permute-start.2 = (f32[32,32,128]{2,1,0:T(8,128)S(1)}, f32[32,32,128]{2,1,0:T(8,128)S(1)}, u32[]{:S(2)}, u32[]{:S(2)}) collective-permute-start(f32[32,32,128]{2,1,0:T(8,128)S(1)} %shard_map.119), channel_id=1, source_target_pairs={{0,4},{1,5},{2,6},{3,7},{4,0},{5,1},{6,2},{7,3},{8,12},{9,13},{10,... | collective-permute-start | bytes 1572872 | tf_op jit(solution)/shard_map/ppermute | solution.py:340

commit v3 on v2

--- a/solution.py
+++ b/solution.py
@@ -126,15 +126,14 @@
     return mid, hdot(hdot(large_ref[0], large_ref[1]), large_ref[2])
 
 
-def prep_send(small_ref, large_ref, masks_ref, where_ref, high_ref, mid_ref, low_ref, built_ref, sems):
+def parts_of(ref):
+    return ref.at[:, :, :512], ref.at[:, :, 512:640], ref.at[:, :, 640:]
+
+
+def prep_send(small_ref, large_ref, masks_ref, where_ref, out_ref):
     mid, low = merged(small_ref, large_ref)
-    refs = (small_ref, large_ref, masks_ref, where_ref, built_ref, mid_ref, low_ref)
-    copies = [pltpu.make_async_copy(built_ref.at[slot], high_ref.at[slot], sems.at[slot]) for slot in range(2)]
     for slot in range(2):
-        prep_block(refs, slot + 1, slot, mid, low)
-        copies[slot].start()
-    for copy in copies:
-        copy.wait()
+        prep_block((small_ref, large_ref, masks_ref, where_ref) + parts_of(out_ref), slot + 1, slot, mid, low)
 
 
 def prep_keep(*refs):
@@ -233,16 +232,12 @@
     return store
 
 
-def send_kernel(early_ref, got_ref, late_ref, high_ref, mid_ref, low_ref, out_ref, first_ref, second_ref, held_ref, sems):
+def send_kernel(early_ref, got_ref, late_ref, built_ref, out_ref, first_ref, second_ref):
     fields = (early_ref, got_ref, late_ref)
-    copies = [pltpu.make_async_copy(high_ref.at[slot], held_ref.at[slot], sems.at[slot]) for slot in range(2)]
-    for copy in copies:
-        copy.start()
-    low_mid(reader(fields, 0), pair_of(mid_ref, 0), pair_of(low_ref, 0), writer(first_ref))
-    low_mid(reader(fields, 1), pair_of(mid_ref, 1), pair_of(low_ref, 1), writer(second_ref))
-    for copy in copies:
-        copy.wait()
-    high_step((first_ref, second_ref), (pair_of(held_ref, 0), pair_of(held_ref, 1)), out_ref)
+    high_ref, mid_ref, low_ref = parts_of(built_ref)
+    for slot, half_ref in enumerate((first_ref, second_ref)):
+        low_mid(reader(fields, slot), pair_of(mid_ref, slot), pair_of(low_ref, slot), writer(half_ref))
+    high_step((first_ref, second_ref), (pair_of(high_ref, 0), pair_of(high_ref, 1)), out_ref)
 
 
 def keep_kernel(early_ref, got_ref, late_ref, high_ref, mid_ref, low_ref, final_ref, out_ref, first_ref):
@@ -274,17 +269,13 @@
     return pl.BlockSpec(memory_space=pltpu.SMEM)
 
 
-def call(body, ins, outs, scratch=(), smem=(), far_in=(), far_out=(), copies=0):
-    far = pl.BlockSpec(memory_space=pltpu.HBM)
-    held = [pltpu.VMEM(s, t) for s, t in scratch]
-    if copies:
-        held.append(pltpu.SemaphoreType.DMA((copies,)))
+def call(body, ins, outs, scratch=(), smem=()):
     return pl.pallas_call(
         body,
-        in_specs=[sm() if i in smem else far if i in far_in else vm() for i in range(ins)],
-        out_specs=[far if i in far_out else vm() for i in range(len(outs))],
+        in_specs=[sm() if i in smem else vm() for i in range(ins)],
+        out_specs=[vm() for _ in outs],
         out_shape=[jax.ShapeDtypeStruct(s, t) for s, t in outs],
-        scratch_shapes=held,
+        scratch_shapes=[pltpu.VMEM(s, t) for s, t in scratch],
         compiler_params=pltpu.CompilerParams(vmem_limit_bytes=16 * 2**20),
     )
 
@@ -323,22 +314,18 @@
     early = lax.all_to_all(
         early.reshape(XY, 8 * EARLY, width), ("x", "y"), split_axis=0, concat_axis=0, tiled=True
     ).reshape(XY, 4, 2, EARLY, width)
-    prepared = [((2, 2, 512, 256), BF16), ((2, 2, 128, 256), BF16), ((2, 2, 128, 256), BF16)]
-    high, mid, low = call(
-        prep_send, 4, prepared, prepared[:1], smem=(2, 3), far_out=(0,), copies=2
-    )(small, large, masks, where)
     early_got = lax.ppermute(early[:, 2:], "zh", swap)
     (both,) = call(add_kernel, 2, [((XY, 2, 2, late, width), F32)])(own, got)
     field = lax.all_to_all(
         both.reshape(XY, 4 * late, width), ("x", "y"), split_axis=0, concat_axis=0, tiled=True
     ).reshape(XY, 2, 2, late, width)
+    operators = ((2, 2, 768, 256), BF16)
+    (built,) = call(prep_send, 4, [operators], smem=(2, 3))(small, large, masks, where)
     whole = ((TOP, MID, width), F32)
     fields = (early, early_got, field)
-    (sent,) = call(
-        send_kernel, 6, [whole], [whole, whole] + prepared[:1], far_in=(3,), copies=2
-    )(*fields, high, mid, low)
+    (sent,) = call(send_kernel, 4, [whole], [whole, whole])(*fields, built)
     arrived = lax.ppermute(sent, "narrow", [(i, i ^ 4) for i in range(8)])
-    prepared = [((1, 2, 512, 256), BF16)] + prepared[1:]
+    prepared = [((1, 2, 512, 256), BF16), ((2, 2, 128, 256), BF16), ((2, 2, 128, 256), BF16)]
     high, mid, low = call(prep_keep, 4, prepared, smem=(2, 3))(small, large, masks, where)
     final, kept = call(keep_kernel, 6, [whole, whole], [whole])(*fields, high, mid, low)
     cotangent = kept + arrived

time: 102 us -> 101 us (level)
  local copies, waits for them, and re-layouts: 5.38 us -> 2.9 us
  starting transfers between devices: 42.4 us -> 44.1 us
    unnamed x29 -> x23, local copies, waits for them, and re-layouts: 5.33 us -> 2.85 us
    ppermute x1, starting transfers between devices: 12.5 us -> 14.3 us  [evolve(): arrived = lax.ppermute(sent, 'narrow', [(i, i ^ 4) for i in range(8)])]
  transfers between devices with their start and end apart: 6 -> 6, of which waited for: 3 -> 3; matrix products, arithmetic and copies ran while one was open for 1% -> 3% of each run, Pallas kernels for 15% -> 14%
where the time goes in v3:
time: 101 us; the launch traced here: 99.6 us
  starting transfers between devices  44.1 us (44%)
  waiting for transfers between devices  29.4 us (29%)
  Pallas kernels  19.8 us (20%)
  local copies, waits for them, and re-layouts  2.9 us (3%)
  other arithmetic  2.51 us (2%)
    ppermute x1, waiting for transfers between devices, evolve(): arrived = lax.ppermute(sent, 'narrow', [(i, i ^ 4) for i in range(8)])  14.5 us
    ppermute x1, starting transfers between devices, evolve(): arrived = lax.ppermute(sent, 'narrow', [(i, i ^ 4) for i in range(8)])  14.3 us
    ppermute x1, waiting for transfers between devices, evolve(): got = lax.ppermute(other, 'zh', swap)  8.4 us
    all_to_all x1, starting transfers between devices, evolve(): lax.all_to_all(amplitudes.reshape(XY, 2 * MID, width), ('x', 'y'), split_...  7.58 us
    ppermute x1, starting transfers between devices, evolve(): got = lax.ppermute(other, 'zh', swap)  6.99 us
    all_to_all x1, waiting for transfers between devices, evolve(): lax.all_to_all(amplitudes.reshape(XY, 2 * MID, width), ('x', 'y'), split_...  6.58 us
    all_to_all x1, starting transfers between devices, evolve(): lax.all_to_all(both.reshape(XY, 4 * late, width), ('x', 'y'), split_axis=...  6.37 us
    ppermute x1, starting transfers between devices, evolve(): early_got = lax.ppermute(early[:, 2:], 'zh', swap)  5.22 us
  transfers between devices with their start and end apart: 6, of which 3 were waited for; matrix products, arithmetic and copies ran while one was open for 3% of the time, Pallas kernels for 14%

profile of v3, /device:TPU:1, one launch (start us, length us, event | category | flops | bytes accessed | tf_op | source)
XLA Modules:
  0.0 99.6 jit_solution(4193621178518905003)
XLA Ops:
  0.6 7.6 %all-to-all-start = ((f32[16,64,128]{2,1,0:T(8,128)}), f32[16,64,128]{2,1,0:T(8,128)S(1)}, u32[]{:S(2)}, u32[]{:S(2)}) async-start(f32[16,64,128]{2,1,0:T(8,128)} %bitcast.34), calls=%async_computation | async-start | bytes 1048576 | tf_op jit(solution)/shard_map/all_to_all | solution.py:296
  8.2 0.9 copy.12
  9.2 1.0 %pad_maximum_fusion = f32[16,2,32,32]{3,2,0,1:T(8,128)S(1)} fusion(f32[6,2,32,32]{3,2,0,1:T(8,128)S(1)} %bitcast.32, f32[4,2,32,32]{3,2,1,0:T(8,128)} %param.11, f32[3,2,32,32]{3,2,1,0:T(8,128)} %param.12, f32[3,2,32,32]{3,2,1,0:T(8,128)} %param.15), kind=kLoop, calls=%fused_computation | loop fusion | flops 98304 | bytes 262144 | tf_op jit(solution)/shard_map/concatenate | solution.py:300
  10.3 0.1 pad_add_fusion.where_ref.refs_3_
  10.4 0.2 maximum_maximum_fusion.small_ref.refs_0_
  10.6 1.4 %shard_map.113.top_ref = bf16[2,2,128,256]{3,2,1,0:T(8,128)(2,1)S(1)} custom-call(f32[16,64,64]{2,1,0:T(8,128)S(1)} %maximum_maximum_fusion.small_ref.refs_0_, s32[3]{0:T(128)S(1)} %pad_add_fusion.where_ref.refs_3_), custom_call_target="tpu_custom_call" | custom-call | tf_op jit(solution)/shard_map/pallas_call | solution.py:308
  12.0 6.6 %all-to-all-done = f32[16,64,128]{2,1,0:T(8,128)S(1)} async-done(((f32[16,64,128]{2,1,0:T(8,128)}), f32[16,64,128]{2,1,0:T(8,128)S(1)}, u32[]{:S(2)}, u32[]{:S(2)}) %all-to-all-start) | async-done | bytes 524320 | tf_op jit(solution)/shard_map/all_to_all | solution.py:296
  18.6 1.4 %shard_map.114 = (f32[16,2,24,128]{3,2,1,0:T(8,128)S(1)}, f32[16,2,24,128]{3,2,1,0:T(8,128)S(1)}, f32[16,4,2,8,128]{4,3,2,1,0:T(8,128)}) custom-call(f32[16,2,32,128]{3,2,1,0:T(8,128)S(1)} %bitcast.31, bf16[2,2,128,256]{3,2,1,0:T(8,128)(2,1)S(1)} %shard_map.113.top_ref), custom_call_target="tpu_custom_call" | custom-call | tf_op jit(solution)/shard_map/pallas_call | solution.py:311
  19.9 3.6 %all-to-all-start.1 = ((f32[16,64,128]{2,1,0:T(8,128)}), f32[16,64,128]{2,1,0:T(8,128)S(1)}, u32[]{:S(2)}, u32[]{:S(2)}) async-start(f32[16,64,128]{2,1,0:T(8,128)} %bitcast.7), calls=%async_computation.1 | async-start | bytes 1048576 | tf_op jit(solution)/shard_map/all_to_all | solution.py:314
  23.5 7.0 %collective-permute-start.1 = (f32[16,2,24,128]{3,2,1,0:T(8,128)S(1)}, f32[16,2,24,128]{3,2,1,0:T(8,128)S(1)}, u32[]{:S(2)}, u32[]{:S(2)}) collective-permute-start(f32[16,2,24,128]{3,2,1,0:T(8,128)S(1)} %get-tuple-element.12), channel_id=1, source_target_pairs={{0,8},{8,0},{1,9},{9,1},{2,10},{10,2},{3,11},{11,3},{4,12},{12,4},... | collective-permute-start | bytes 1179656 | tf_op jit(solution)/shard_map/ppermute | solution.py:313
  30.5 8.4 %collective-permute-done.1.got_ref = f32[16,2,24,128]{3,2,1,0:T(8,128)S(1)} collective-permute-done((f32[16,2,24,128]{3,2,1,0:T(8,128)S(1)}, f32[16,2,24,128]{3,2,1,0:T(8,128)S(1)}, u32[]{:S(2)}, u32[]{:S(2)}) %collective-permute-start.1) | collective-permute-done | bytes 393248 | tf_op jit(solution)/shard_map/ppermute | solution.py:313
  38.9 0.0 copy-start.5
  38.9 0.0 copy-start.6
  38.9 0.9 shard_map.115
  39.9 0.0 all-to-all-done.1
  39.9 0.0 copy-start.7
  39.9 0.0 copy-start.8
  39.9 0.0 copy-start.9
  39.9 6.4 %all-to-all-start.2 = ((f32[16,96,128]{2,1,0:T(8,128)}), f32[16,96,128]{2,1,0:T(8,128)S(1)}, u32[]{:S(2)}, u32[]{:S(2)}) async-start(f32[16,96,128]{2,1,0:T(8,128)} %bitcast.9), calls=%async_computation.2 | async-start | bytes 1572864 | tf_op jit(solution)/shard_map/all_to_all | solution.py:319
  46.2 0.0 copy-done.5
  46.3 0.1 copy.16
  46.4 0.0 copy-done.6
  46.4 0.1 copy.17
  46.6 5.2 %collective-permute-start = (f32[16,2,2,8,128]{4,3,2,1,0:T(8,128)S(1)}, f32[16,2,2,8,128]{4,3,2,1,0:T(8,128)S(1)}, u32[]{:S(2)}, u32[]{:S(2)}) collective-permute-start(f32[16,2,2,8,128]{4,3,2,1,0:T(8,128)S(1)} %slice.22), channel_id=1, source_target_pairs={{0,8},{8,0},{1,9},{9,1},{2,10},{10,2},{3,11},{11,3},{4,12},{12,4},... | collective-permute-start | bytes 786440 | tf_op jit(solution)/shard_map/ppermute | solution.py:317
  51.8 0.0 copy-done.7
  51.8 0.0 copy-done.8
  51.8 0.0 copy-done.9
  51.8 0.1 pad_add_fusion.1.refs_2_.masks_ref
  51.9 0.2 maximum_maximum_fusion.1.refs_1_.large_ref
  52.1 0.0 copy-start
  52.1 4.5 %shard_map.118.built_ref = bf16[2,2,768,256]{3,2,1,0:T(8,128)(2,1)S(1)} custom-call(f32[16,64,64]{2,1,0:T(8,128)S(1)} %maximum_maximum_fusion.small_ref.refs_0_, f32[6,128,128]{2,1,0:T(8,128)S(1)} %maximum_maximum_fusion.1.refs_1_.large_ref, s32[9]{0:T(128)S(1)} %pad_add_fusion.1.refs_2_.masks_ref, s32[3]{0:T(128)S(1)} %pad_add_fusion.where_ref.refs_3_), custom_call_target="tpu_custom_call" | custom-call | tf_op jit(solution)/shard_map/pallas_call | solution.py:323
  56.6 0.0 copy-done
  56.6 0.0 collective-permute-done.got_ref
  56.7 0.0 copy-start.2
  56.7 0.7 copy-done.2
  57.4 0.0 all-to-all-done.2
  57.4 0.0 copy-start.3
  57.4 0.9 copy-done.3
  58.3 0.0 copy-start.1
  58.3 0.0 copy-start.4
  58.3 4.2 %shard_map.119 = f32[32,32,128]{2,1,0:T(8,128)S(1)} custom-call(f32[16,4,2,8,128]{4,3,2,1,0:T(8,128)S(1)} %bitcast.29, f32[16,2,2,8,128]{4,3,2,1,0:T(8,128)S(1)} %copy-done.3, f32[16,2,2,24,128]{4,3,2,1,0:T(8,128)S(1)} %bitcast.26, bf16[2,2,768,256]{3,2,1,0:T(8,128)(2,1)S(1)} %shard_map.118.built_ref), custom_call_target="tpu_custom_call" | custom-call | tf_op jit(solution)/shard_map/pallas_call | solution.py:326
  62.5 14.3 %collective-permute-start.2 = (f32[32,32,128]{2,1,0:T(8,128)S(1)}, f32[32,32,128]{2,1,0:T(8,128)S(1)}, u32[]{:S(2)}, u32[]{:S(2)}) collective-permute-start(f32[32,32,128]{2,1,0:T(8,128)S(1)} %shard_map.119), channel_id=1, source_target_pairs={{0,4},{1,5},{2,6},{3,7},{4,0},{5,1},{6,2},{7,3},{8,12},{9,13},{10,... | collective-permute-start | bytes 1572872 | tf_op jit(solution)/shard_map/ppermute | solution.py:327
  76.9 0.0 copy-done.1
  76.9 2.9 %shard_map.116 = (bf16[1,2,512,256]{3,2,1,0:T(8,128)(2,1)S(1)}, bf16[2,2,128,256]{3,2,1,0:T(8,128)(2,1)S(1)}, bf16[2,2,128,256]{3,2,1,0:T(8,128)(2,1)S(1)}) custom-call(f32[16,64,64]{2,1,0:T(8,128)S(1)} %maximum_maximum_fusion.small_ref.refs_0_, f32[6,128,128]{2,1,0:T(8,128)S(1)} %copy-done.1, s32[9]{0:T(128)S(1)} %pad_add_fusion.1.refs_2_.masks_ref, ...), custom_call_target="tpu_custom_call" | custom-call | tf_op jit(solution)/shard_map/pallas_call | solution.py:329
  79.8 0.0 copy-done.4
  79.8 4.5 %shard_map.117 = (f32[32,32,128]{2,1,0:T(8,128)}, f32[32,32,128]{2,1,0:T(8,128)S(1)}) custom-call(f32[16,4,2,8,128]{4,3,2,1,0:T(8,128)S(1)} %bitcast.30, f32[16,2,2,8,128]{4,3,2,1,0:T(8,128)S(1)} %copy-done.4, f32[16,2,2,24,128]{4,3,2,1,0:T(8,128)S(1)} %bitcast.27, bf16[1,2,512,256]{3,2,1,0:T(8,128)(2,1)S(1)} %get-tuple-element.13.high_ref, ...), custom_call_target="tpu_custom_call" | custom-call | tf_op jit(solution)/shard_map/pallas_call | solution.py:330
  84.3 14.5 %collective-permute-done.2 = f32[32,32,128]{2,1,0:T(8,128)S(1)} collective-permute-done((f32[32,32,128]{2,1,0:T(8,128)S(1)}, f32[32,32,128]{2,1,0:T(8,128)S(1)}, u32[]{:S(2)}, u32[]{:S(2)}) %collective-permute-start.2) | collective-permute-done | bytes 524320 | tf_op jit(solution)/shard_map/ppermute | solution.py:327
  98.7 0.9 add.15
  (5 shorter events, 0.1 us)
Async XLA Ops:
  0.6 18.0 %all-to-all-start = ((f32[16,64,128]{2,1,0:T(8,128)}), f32[16,64,128]{2,1,0:T(8,128)S(1)}, u32[]{:S(2)}, u32[]{:S(2)}) async-start(f32[16,64,128]{2,1,0:T(8,128)} %bitcast.34), calls=%async_computation | async-start | bytes 1048576 | tf_op jit(solution)/shard_map/all_to_all | solution.py:296
  19.9 19.9 %all-to-all-start.1 = ((f32[16,64,128]{2,1,0:T(8,128)}), f32[16,64,128]{2,1,0:T(8,128)S(1)}, u32[]{:S(2)}, u32[]{:S(2)}) async-start(f32[16,64,128]{2,1,0:T(8,128)} %bitcast.7), calls=%async_computation.1 | async-start | bytes 1048576 | tf_op jit(solution)/shard_map/all_to_all | solution.py:314
  23.5 15.4 %collective-permute-start.1 = (f32[16,2,24,128]{3,2,1,0:T(8,128)S(1)}, f32[16,2,24,128]{3,2,1,0:T(8,128)S(1)}, u32[]{:S(2)}, u32[]{:S(2)}) collective-permute-start(f32[16,2,24,128]{3,2,1,0:T(8,128)S(1)} %get-tuple-element.12), channel_id=1, source_target_pairs={{0,8},{8,0},{1,9},{9,1},{2,10},{10,2},{3,11},{11,3},{4,12},{12,4},... | collective-permute-start | bytes 1179656 | tf_op jit(solution)/shard_map/ppermute | solution.py:313
  38.9 7.3 %copy-start.5 = (f32[3,2,64,64]{3,2,1,0:T(8,128)S(1)}, f32[3,2,64,64]{3,2,1,0:T(8,128)}, u32[]{:S(2)}) copy-start(f32[3,2,64,64]{3,2,1,0:T(8,128)} %param.13) | copy-start | bytes 294916
  38.9 7.5 %copy-start.6 = (f32[3,2,64,64]{3,2,1,0:T(8,128)S(1)}, f32[3,2,64,64]{3,2,1,0:T(8,128)}, u32[]{:S(2)}) copy-start(f32[3,2,64,64]{3,2,1,0:T(8,128)} %param.16) | copy-start | bytes 294916
  39.9 11.9 %copy-start.7 = (s32[3]{0:T(128)S(1)}, s32[3]{0:T(128)}, u32[]{:S(2)}) copy-start(s32[3]{0:T(128)} %param.19) | copy-start | bytes 40
  39.9 11.9 %copy-start.8 = (s32[3]{0:T(128)S(1)}, s32[3]{0:T(128)}, u32[]{:S(2)}) copy-start(s32[3]{0:T(128)} %param.18) | copy-start | bytes 40
  39.9 11.9 %copy-start.9 = (s32[3]{0:T(128)S(1)}, s32[3]{0:T(128)}, u32[]{:S(2)}) copy-start(s32[3]{0:T(128)} %param.17) | copy-start | bytes 40
  39.9 17.5 %all-to-all-start.2 = ((f32[16,96,128]{2,1,0:T(8,128)}), f32[16,96,128]{2,1,0:T(8,128)S(1)}, u32[]{:S(2)}, u32[]{:S(2)}) async-start(f32[16,96,128]{2,1,0:T(8,128)} %bitcast.9), calls=%async_computation.2 | async-start | bytes 1572864 | tf_op jit(solution)/shard_map/all_to_all | solution.py:319
  46.6 10.1 %collective-permute-start = (f32[16,2,2,8,128]{4,3,2,1,0:T(8,128)S(1)}, f32[16,2,2,8,128]{4,3,2,1,0:T(8,128)S(1)}, u32[]{:S(2)}, u32[]{:S(2)}) collective-permute-start(f32[16,2,2,8,128]{4,3,2,1,0:T(8,128)S(1)} %slice.22), channel_id=1, source_target_pairs={{0,8},{8,0},{1,9},{9,1},{2,10},{10,2},{3,11},{11,3},{4,12},{12,4},... | collective-permute-start | bytes 786440 | tf_op jit(solution)/shard_map/ppermute | solution.py:317
  52.1 4.6 %copy-start = (f32[6,128,128]{2,1,0:T(8,128)}, f32[6,128,128]{2,1,0:T(8,128)S(1)}, u32[]{:S(2)}) copy-start(f32[6,128,128]{2,1,0:T(8,128)S(1)} %maximum_maximum_fusion.1.refs_1_.large_ref) | copy-start | bytes 1179652
  56.7 0.7 copy-start.2
  57.4 1.0 copy-start.3
  58.3 18.6 %copy-start.1 = (f32[6,128,128]{2,1,0:T(8,128)S(1)}, f32[6,128,128]{2,1,0:T(8,128)}, u32[]{:S(2)}) copy-start(f32[6,128,128]{2,1,0:T(8,128)} %copy-done) | copy-start | bytes 1179652
  58.3 21.5 %copy-start.4 = (f32[16,2,2,8,128]{4,3,2,1,0:T(8,128)S(1)}, f32[16,2,2,8,128]{4,3,2,1,0:T(8,128)}, u32[]{:S(2)}) copy-start(f32[16,2,2,8,128]{4,3,2,1,0:T(8,128)} %copy-done.2) | copy-start | bytes 786436
  62.5 36.2 %collective-permute-start.2 = (f32[32,32,128]{2,1,0:T(8,128)S(1)}, f32[32,32,128]{2,1,0:T(8,128)S(1)}, u32[]{:S(2)}, u32[]{:S(2)}) collective-permute-start(f32[32,32,128]{2,1,0:T(8,128)S(1)} %shard_map.119), channel_id=1, source_target_pairs={{0,4},{1,5},{2,6},{3,7},{4,0},{5,1},{6,2},{7,3},{8,12},{9,13},{10,... | collective-permute-start | bytes 1572872 | tf_op jit(solution)/shard_map/ppermute | solution.py:327

commit v4 on v3

--- a/solution.py
+++ b/solution.py
@@ -86,14 +86,16 @@
         )
 
 
-def spread_high(matrix, scale):
-    row, col = iotas((TOP, 8 * TOP))
-    wide = hdot(matrix[:, :TOP], jnp.where(row == col // 8, 1.0, 0.0))
-    row, col = iotas((8 * TOP, TOP))
-    pick = jnp.where(col == row // 8, 1.0, 0.0)
-    row, col = iotas((8 * TOP, 8 * TOP))
-    same = jnp.where(row % 8 == col % 8, scale, 0.0)
-    return jnp.concatenate([hdot(pick, wide[:TOP]) * same, hdot(pick, wide[TOP:]) * same], axis=0)
+def three_passes(matrices):
+    columns = 3 * TOP * len(matrices)
+    row, col = iotas((TOP, columns))
+    wide = sum(
+        hdot(matrix[:, :TOP], jnp.where((col % TOP == row) & (col // (3 * TOP) == index), 1.0, 0.0))
+        for index, matrix in enumerate(matrices)
+    )
+    high = wide.astype(BF16).astype(F32)
+    _, col = iotas(wide.shape)
+    return jnp.where(col // TOP % 3 == 1, wide - high, high).astype(BF16)
 
 
 def spread_mid(matrix):
@@ -107,18 +109,20 @@
 
 
 def prep_block(refs, block, slot, mid, low):
-    small_ref, large_ref, masks_ref, where_ref, high_ref, mid_ref, low_ref = refs
+    small_ref, large_ref, masks_ref, where_ref, built_ref = refs
     flip, phase = masks_ref[block], masks_ref[BLOCKS + block]
     source = where_ref[0] if block == 1 else jnp.bitwise_xor(where_ref[0], where_ref[2])
     scale = sign_of(jnp.bitwise_and(source, masks_ref[2 * BLOCKS + block]))
+    fold = fold_left(2 * MID, flip // LOW % MID, phase // LOW % MID)
+    full = fold_right(2 * LOW, flip % LOW, phase % LOW)
+    put_pair(built_ref, slot, hdot(fold, hdot(small_ref[13 + block], mid)), hdot(hdot(low, large_ref[3 + block]), full))
     fold = fold_left(2 * TOP, flip // (MID * LOW), phase // (MID * LOW))
-    high = hdot(fold, hdot(small_ref[8 + 2 * block], small_ref[7 + 2 * block]))
-    put(high_ref, slot, spread_high(high, scale))
-    fold = fold_left(2 * MID, flip // LOW % MID, phase // LOW % MID)
-    put(mid_ref, slot, spread_mid(hdot(fold, hdot(small_ref[13 + block], mid))))
-    fold = fold_right(2 * LOW, flip % LOW, phase % LOW)
-    full = hdot(hdot(low, large_ref[3 + block]), fold)
-    put(low_ref, slot, jnp.concatenate([full, times_i(full)], axis=1))
+    return hdot(fold, hdot(small_ref[8 + 2 * block], small_ref[7 + 2 * block])) * scale
+
+
+def put_pair(ref, slot, mid, low):
+    put(ref.at[:, :, : 4 * MID], slot, spread_mid(mid))
+    put(ref.at[:, :, 4 * MID :], slot, jnp.concatenate([low, times_i(low)], axis=1))
 
 
 def merged(small_ref, large_ref):
@@ -126,21 +130,22 @@
     return mid, hdot(hdot(large_ref[0], large_ref[1]), large_ref[2])
 
 
-def parts_of(ref):
-    return ref.at[:, :, :512], ref.at[:, :, 512:640], ref.at[:, :, 640:]
-
-
-def prep_send(small_ref, large_ref, masks_ref, where_ref, out_ref):
+def parts_of(ref, slot):
+    pair = ref.at[slot]
+    return tuple((pair[0, rows], pair[1, rows]) for rows in (slice(0, 4 * MID), slice(4 * MID, 8 * MID)))
+
+
+def prep_send(small_ref, large_ref, masks_ref, where_ref, high_ref, built_ref):
+    refs = (small_ref, large_ref, masks_ref, where_ref, built_ref)
     mid, low = merged(small_ref, large_ref)
-    for slot in range(2):
-        prep_block((small_ref, large_ref, masks_ref, where_ref) + parts_of(out_ref), slot + 1, slot, mid, low)
-
-
-def prep_keep(*refs):
-    mid, low = merged(*refs[:2])
-    prep_block(refs, 0, 0, mid, low)
-    put(refs[5], 1, spread_mid(mid))
-    put(refs[6], 1, jnp.concatenate([low, times_i(low)], axis=1))
+    high_ref[...] = three_passes([prep_block(refs, slot + 1, slot, mid, low) for slot in range(2)])
+
+
+def prep_keep(small_ref, large_ref, masks_ref, where_ref, high_ref, built_ref):
+    refs = (small_ref, large_ref, masks_ref, where_ref, built_ref)
+    mid, low = merged(small_ref, large_ref)
+    high_ref[...] = three_passes([prep_block(refs, 0, 0, mid, low)])
+    put_pair(built_ref, 1, mid, low)
 
 
 def two_streams(out_ref, first, value):
@@ -191,25 +196,18 @@
         store(group, jnp.concatenate([done[:, : 2 * LOW], done[:, 2 * LOW :]], axis=0))
 
 
-def pair_of(ref, index):
-    return ref[index, 0], ref[index, 1]
-
-
-def high_step(sources, matrices, out_ref):
-    rows = 8 * TOP
-    for pair in range(2):
-        total = None
-        for source_ref, matrix in zip(sources, matrices):
-            parts = [
-                source_ref[:, 16 * pair + 8 * half : 16 * pair + 8 * half + 8, :].reshape(rows, 2 * LOW)
-                for half in range(2)
-            ]
-            done = dot3(matrix, split(jnp.concatenate(parts, axis=1)))
-            total = done if total is None else total + done
+def high_step(sources, matrix_ref, out_ref):
+    matrix = matrix_ref[...]
+    for item in range(0, MID, 2):
+        right = []
+        for source_ref in sources:
+            parts = [source_ref[pl.ds(item + half, TOP, stride=MID), :] for half in range(2)]
+            high, low = split(jnp.concatenate(parts, axis=1))
+            right += [high, high, low]
+        total = jnp.dot(matrix, jnp.concatenate(right, axis=0), preferred_element_type=F32)
         for half in range(2):
             part = total[:, 2 * LOW * half : 2 * LOW * (half + 1)]
-            value = part[:rows] + times_i(part[rows:])
-            out_ref[:, 16 * pair + 8 * half : 16 * pair + 8 * half + 8, :] = value.reshape(TOP, 8, 2 * LOW)
+            out_ref[pl.ds(item + half, TOP, stride=MID), :] = part[:TOP] + times_i(part[TOP:])
 
 
 def reader(fields, stream):
@@ -227,24 +225,26 @@
 
 def writer(ref):
     def store(group, value):
-        ref[8 * group : 8 * group + 8] = value.reshape(8, MID, 2 * LOW)
+        ref[8 * MID * group : 8 * MID * (group + 1)] = value
 
     return store
 
 
-def send_kernel(early_ref, got_ref, late_ref, built_ref, out_ref, first_ref, second_ref):
+def send_kernel(early_ref, got_ref, late_ref, high_ref, built_ref, out_ref, first_ref, second_ref):
     fields = (early_ref, got_ref, late_ref)
-    high_ref, mid_ref, low_ref = parts_of(built_ref)
     for slot, half_ref in enumerate((first_ref, second_ref)):
-        low_mid(reader(fields, slot), pair_of(mid_ref, slot), pair_of(low_ref, slot), writer(half_ref))
-    high_step((first_ref, second_ref), (pair_of(high_ref, 0), pair_of(high_ref, 1)), out_ref)
-
-
-def keep_kernel(early_ref, got_ref, late_ref, high_ref, mid_ref, low_ref, final_ref, out_ref, first_ref):
+        mid, low = parts_of(built_ref, slot)
+        low_mid(reader(fields, slot), mid, low, writer(half_ref))
+    high_step((first_ref, second_ref), high_ref, out_ref)
+
+
+def keep_kernel(early_ref, got_ref, late_ref, high_ref, built_ref, final_ref, out_ref, first_ref):
     fields = (early_ref, got_ref, late_ref)
-    low_mid(reader(fields, 1), pair_of(mid_ref, 0), pair_of(low_ref, 0), writer(first_ref))
-    high_step((first_ref,), (pair_of(high_ref, 0),), out_ref)
-    low_mid(reader(fields, 0), pair_of(mid_ref, 1), pair_of(low_ref, 1), writer(final_ref))
+    mid, low = parts_of(built_ref, 0)
+    low_mid(reader(fields, 1), mid, low, writer(first_ref))
+    high_step((first_ref,), high_ref, out_ref)
+    mid, low = parts_of(built_ref, 1)
+    low_mid(reader(fields, 0), mid, low, writer(final_ref))
 
 
 def real_form(matrix):
@@ -319,17 +319,15 @@
     field = lax.all_to_all(
         both.reshape(XY, 4 * late, width), ("x", "y"), split_axis=0, concat_axis=0, tiled=True
     ).reshape(XY, 2, 2, late, width)
-    operators = ((2, 2, 768, 256), BF16)
-    (built,) = call(prep_send, 4, [operators], smem=(2, 3))(small, large, masks, where)
-    whole = ((TOP, MID, width), F32)
+    built = ((2, 2, 8 * MID, 256), BF16)
+    prepared = call(prep_send, 4, [((2 * TOP, 6 * TOP), BF16), built], smem=(2, 3))(small, large, masks, where)
+    whole = ((TOP * MID, width), F32)
     fields = (early, early_got, field)
-    (sent,) = call(send_kernel, 4, [whole], [whole, whole])(*fields, built)
+    (sent,) = call(send_kernel, 5, [whole], [whole, whole])(*fields, *prepared)
     arrived = lax.ppermute(sent, "narrow", [(i, i ^ 4) for i in range(8)])
-    prepared = [((1, 2, 512, 256), BF16), ((2, 2, 128, 256), BF16), ((2, 2, 128, 256), BF16)]
-    high, mid, low = call(prep_keep, 4, prepared, smem=(2, 3))(small, large, masks, where)
-    final, kept = call(keep_kernel, 6, [whole, whole], [whole])(*fields, high, mid, low)
-    cotangent = kept + arrived
-    return final.reshape(TOP * MID, width), cotangent.reshape(TOP * MID, width)
+    prepared = call(prep_keep, 4, [((2 * TOP, 3 * TOP), BF16), built], smem=(2, 3))(small, large, masks, where)
+    final, kept = call(keep_kernel, 5, [whole, whole], [whole])(*fields, *prepared)
+    return final, kept + arrived
 
 
 def solution(mesh):

time: 101 us -> 99.7 us (0.987)
  waiting for transfers between devices: 29.4 us -> 32.1 us
  Pallas kernels: 19.8 us -> 17.5 us
  other arithmetic: 2.51 us -> 1.48 us
    pallas_call x4, Pallas kernels: 16.1 us -> 13.8 us  [the longest x1 4.6 us: evolve(): call(keep_kernel, 5, [whole, whole], [whole])(*fields, *prepared)]
    unnamed x23 -> x21, local copies, waits for them, and re-layouts: 2.85 us -> 2.03 us
  transfers between devices with their start and end apart: 6 -> 6, of which waited for: 3 -> 5; matrix products, arithmetic and copies ran while one was open for 3% -> 1% of each run, Pallas kernels for 14% -> 12%
where the time goes in v4:
time: 99.7 us; the launch traced here: 98.7 us
  starting transfers between devices  44.6 us (45%)
  waiting for transfers between devices  32.1 us (32%)
  Pallas kernels  17.5 us (18%)
  local copies, waits for them, and re-layouts  2.08 us (2%)
  other arithmetic  1.48 us (1%)
    ppermute x1, waiting for transfers between devices, evolve(): arrived = lax.ppermute(sent, 'narrow', [(i, i ^ 4) for i in range(8)])  15.1 us
    ppermute x1, starting transfers between devices, evolve(): arrived = lax.ppermute(sent, 'narrow', [(i, i ^ 4) for i in range(8)])  14.8 us
    ppermute x1, waiting for transfers between devices, evolve(): got = lax.ppermute(other, 'zh', swap)  8.4 us
    all_to_all x1, starting transfers between devices, evolve(): lax.all_to_all(amplitudes.reshape(XY, 2 * MID, width), ('x', 'y'), split_...  7.72 us
    all_to_all x1, waiting for transfers between devices, evolve(): lax.all_to_all(amplitudes.reshape(XY, 2 * MID, width), ('x', 'y'), split_...  7.51 us
    ppermute x1, starting transfers between devices, evolve(): got = lax.ppermute(other, 'zh', swap)  6.99 us
    all_to_all x1, starting transfers between devices, evolve(): lax.all_to_all(both.reshape(XY, 4 * late, width), ('x', 'y'), split_axis=...  6.36 us
    ppermute x1, starting transfers between devices, evolve(): early_got = lax.ppermute(early[:, 2:], 'zh', swap)  5.22 us
  transfers between devices with their start and end apart: 6, of which 5 were waited for; matrix products, arithmetic and copies ran while one was open for 1% of the time, Pallas kernels for 12%

profile of v4, /device:TPU:1, one launch (start us, length us, event | category | flops | bytes accessed | tf_op | source)
XLA Modules:
  0.0 98.7 jit_solution(74033445278064499)
XLA Ops:
  0.6 0.0 copy-start
  0.6 7.7 %all-to-all-start = ((f32[16,64,128]{2,1,0:T(8,128)}), f32[16,64,128]{2,1,0:T(8,128)S(1)}, u32[]{:S(2)}, u32[]{:S(2)}) async-start(f32[16,64,128]{2,1,0:T(8,128)} %bitcast.31), calls=%async_computation | async-start | bytes 1048576 | tf_op jit(solution)/shard_map/all_to_all | solution.py:296
  8.4 0.0 copy-done
  8.4 0.0 copy-start.3
  8.4 0.0 copy-start.4
  8.4 0.0 copy-start.5
  8.4 0.8 copy-done.3
  9.3 0.1 copy-done.4
  9.3 0.0 copy-done.5
  9.5 0.1 pad_add_fusion.where_ref
  9.6 0.2 maximum_maximum_fusion.small_ref
  9.8 1.4 %shard_map.113.top_ref = bf16[2,2,128,256]{3,2,1,0:T(8,128)(2,1)S(1)} custom-call(f32[16,64,64]{2,1,0:T(8,128)S(1)} %maximum_maximum_fusion.small_ref, s32[3]{0:T(128)S(1)} %pad_add_fusion.where_ref), custom_call_target="tpu_custom_call" | custom-call | tf_op jit(solution)/shard_map/pallas_call | solution.py:308
  11.2 7.5 %all-to-all-done = f32[16,64,128]{2,1,0:T(8,128)S(1)} async-done(((f32[16,64,128]{2,1,0:T(8,128)}), f32[16,64,128]{2,1,0:T(8,128)S(1)}, u32[]{:S(2)}, u32[]{:S(2)}) %all-to-all-start) | async-done | bytes 524320 | tf_op jit(solution)/shard_map/all_to_all | solution.py:296
  18.7 1.4 %shard_map.114 = (f32[16,2,24,128]{3,2,1,0:T(8,128)S(1)}, f32[16,2,24,128]{3,2,1,0:T(8,128)S(1)}, f32[16,4,2,8,128]{4,3,2,1,0:T(8,128)}) custom-call(f32[16,2,32,128]{3,2,1,0:T(8,128)S(1)} %bitcast.29, bf16[2,2,128,256]{3,2,1,0:T(8,128)(2,1)S(1)} %shard_map.113.top_ref), custom_call_target="tpu_custom_call" | custom-call | tf_op jit(solution)/shard_map/pallas_call | solution.py:311
  20.1 3.6 %all-to-all-start.1 = ((f32[16,64,128]{2,1,0:T(8,128)}), f32[16,64,128]{2,1,0:T(8,128)S(1)}, u32[]{:S(2)}, u32[]{:S(2)}) async-start(f32[16,64,128]{2,1,0:T(8,128)} %bitcast.7), calls=%async_computation.1 | async-start | bytes 1048576 | tf_op jit(solution)/shard_map/all_to_all | solution.py:314
  23.7 7.0 %collective-permute-start.1 = (f32[16,2,24,128]{3,2,1,0:T(8,128)S(1)}, f32[16,2,24,128]{3,2,1,0:T(8,128)S(1)}, u32[]{:S(2)}, u32[]{:S(2)}) collective-permute-start(f32[16,2,24,128]{3,2,1,0:T(8,128)S(1)} %get-tuple-element.13), channel_id=1, source_target_pairs={{0,8},{8,0},{1,9},{9,1},{2,10},{10,2},{3,11},{11,3},{4,12},{12,4},... | collective-permute-start | bytes 1179656 | tf_op jit(solution)/shard_map/ppermute | solution.py:313
  30.7 8.4 %collective-permute-done.1.got_ref = f32[16,2,24,128]{3,2,1,0:T(8,128)S(1)} collective-permute-done((f32[16,2,24,128]{3,2,1,0:T(8,128)S(1)}, f32[16,2,24,128]{3,2,1,0:T(8,128)S(1)}, u32[]{:S(2)}, u32[]{:S(2)}) %collective-permute-start.1) | collective-permute-done | bytes 393248 | tf_op jit(solution)/shard_map/ppermute | solution.py:313
  39.1 0.9 shard_map.115
  40.0 0.0 all-to-all-done.1
  40.0 0.0 copy-start.1
  40.0 6.4 %all-to-all-start.2 = ((f32[16,96,128]{2,1,0:T(8,128)}), f32[16,96,128]{2,1,0:T(8,128)S(1)}, u32[]{:S(2)}, u32[]{:S(2)}) async-start(f32[16,96,128]{2,1,0:T(8,128)} %bitcast.9), calls=%async_computation.2 | async-start | bytes 1572864 | tf_op jit(solution)/shard_map/all_to_all | solution.py:319
  46.4 0.0 copy-done.1
  46.4 0.0 copy-start.2
  46.4 0.1 copy.16
  46.5 0.8 copy-done.2
  47.3 0.1 copy.17
  47.5 0.0 copy-start.6
  47.5 0.0 copy-start.7
  47.5 0.0 copy-start.8
  47.5 5.2 %collective-permute-start = (f32[16,2,2,8,128]{4,3,2,1,0:T(8,128)S(1)}, f32[16,2,2,8,128]{4,3,2,1,0:T(8,128)S(1)}, u32[]{:S(2)}, u32[]{:S(2)}) collective-permute-start(f32[16,2,2,8,128]{4,3,2,1,0:T(8,128)S(1)} %slice.22), channel_id=1, source_target_pairs={{0,8},{8,0},{1,9},{9,1},{2,10},{10,2},{3,11},{11,3},{4,12},{12,4},... | collective-permute-start | bytes 786440 | tf_op jit(solution)/shard_map/ppermute | solution.py:317
  52.7 0.0 copy-done.6
  52.7 0.0 copy-done.7
  52.7 0.0 copy-done.8
  52.7 0.1 pad_add_fusion.1.masks_ref
  52.9 0.2 maximum_maximum_fusion.1.large_ref
  53.0 3.0 %shard_map.118 = (bf16[64,192]{1,0:T(8,128)(2,1)S(1)}, bf16[2,2,256,256]{3,2,1,0:T(8,128)(2,1)S(1)}) custom-call(f32[16,64,64]{2,1,0:T(8,128)S(1)} %maximum_maximum_fusion.small_ref, f32[6,128,128]{2,1,0:T(8,128)S(1)} %maximum_maximum_fusion.1.large_ref, s32[9]{0:T(128)S(1)} %pad_add_fusion.1.masks_ref, s32[3]{0:T(128)S(1)} %pad_add_fusion.where_ref), custom_call_target="tpu_custom_call" | custom-call | tf_op jit(solution)/shard_map/pallas_call | solution.py:323
  56.1 0.7 collective-permute-done.got_ref
  56.7 0.4 all-to-all-done.2
  57.2 4.1 %shard_map.119 = f32[1024,128]{1,0:T(8,128)S(1)} custom-call(f32[16,4,2,8,128]{4,3,2,1,0:T(8,128)S(1)} %bitcast.27, f32[16,2,2,8,128]{4,3,2,1,0:T(8,128)S(1)} %collective-permute-done.got_ref, f32[16,2,2,24,128]{4,3,2,1,0:T(8,128)S(1)} %bitcast.24, bf16[64,192]{1,0:T(8,128)(2,1)S(1)} %get-tuple-element.18.high_ref, ...), custom_call_target="tpu_custom_call" | custom-call | tf_op jit(solution)/shard_map/pallas_call | solution.py:326
  61.3 14.8 %collective-permute-start.2 = (f32[1024,128]{1,0:T(8,128)S(1)}, f32[1024,128]{1,0:T(8,128)S(1)}, u32[]{:S(2)}, u32[]{:S(2)}) collective-permute-start(f32[1024,128]{1,0:T(8,128)S(1)} %shard_map.119), channel_id=1, source_target_pairs={{0,4},{1,5},{2,6},{3,7},{4,0},{5,1},{6,2},{7,3},{8,12},{9,13},{10,... | collective-permute-start | bytes 1572872 | tf_op jit(solution)/shard_map/ppermute | solution.py:327
  76.0 2.1 %shard_map.116 = (bf16[64,96]{1,0:T(8,128)(2,1)S(1)}, bf16[2,2,256,256]{3,2,1,0:T(8,128)(2,1)S(1)}) custom-call(f32[16,64,64]{2,1,0:T(8,128)S(1)} %maximum_maximum_fusion.small_ref, f32[6,128,128]{2,1,0:T(8,128)S(1)} %maximum_maximum_fusion.1.large_ref, s32[9]{0:T(128)S(1)} %pad_add_fusion.1.masks_ref, s32[3]{0:T(128)S(1)} %pad_add_fusion.where_ref), custom_call_target="tpu_custom_call" | custom-call | tf_op jit(solution)/shard_map/pallas_call | solution.py:328
  78.2 4.6 %shard_map.117 = (f32[1024,128]{1,0:T(8,128)}, f32[1024,128]{1,0:T(8,128)S(1)}) custom-call(f32[16,4,2,8,128]{4,3,2,1,0:T(8,128)S(1)} %bitcast.28, f32[16,2,2,8,128]{4,3,2,1,0:T(8,128)S(1)} %collective-permute-done.got_ref, f32[16,2,2,24,128]{4,3,2,1,0:T(8,128)S(1)} %bitcast.25, bf16[64,96]{1,0:T(8,128)(2,1)S(1)} %get-tuple-element.14.high_ref, ...), custom_call_target="tpu_custom_call" | custom-call | tf_op jit(solution)/shard_map/pallas_call | solution.py:329
  82.8 15.1 %collective-permute-done.2 = f32[1024,128]{1,0:T(8,128)S(1)} collective-permute-done((f32[1024,128]{1,0:T(8,128)S(1)}, f32[1024,128]{1,0:T(8,128)S(1)}, u32[]{:S(2)}, u32[]{:S(2)}) %collective-permute-start.2) | collective-permute-done | bytes 524320 | tf_op jit(solution)/shard_map/ppermute | solution.py:327
  97.8 0.8 add.15
  (7 shorter events, 0.2 us)
Async XLA Ops:
  0.6 7.7 %copy-start = (f32[3,2,2,32,32]{4,3,2,1,0:T(8,128)S(1)}, f32[3,2,2,32,32]{4,3,2,1,0:T(8,128)}, u32[]{:S(2)}) copy-start(f32[3,2,2,32,32]{4,3,2,1,0:T(8,128)} %param.14) | copy-start | bytes 147460
  0.6 18.1 %all-to-all-start = ((f32[16,64,128]{2,1,0:T(8,128)}), f32[16,64,128]{2,1,0:T(8,128)S(1)}, u32[]{:S(2)}, u32[]{:S(2)}) async-start(f32[16,64,128]{2,1,0:T(8,128)} %bitcast.31), calls=%async_computation | async-start | bytes 1048576 | tf_op jit(solution)/shard_map/all_to_all | solution.py:296
  8.4 0.9 copy-start.3
  8.4 0.9 copy-start.4
  8.4 1.0 %copy-start.5 = (f32[3,2,32,32]{3,2,1,0:T(8,128)S(1)}, f32[3,2,32,32]{3,2,1,0:T(8,128)}, u32[]{:S(2)}) copy-start(f32[3,2,32,32]{3,2,1,0:T(8,128)} %param.15) | copy-start | bytes 73732
  20.1 19.9 %all-to-all-start.1 = ((f32[16,64,128]{2,1,0:T(8,128)}), f32[16,64,128]{2,1,0:T(8,128)S(1)}, u32[]{:S(2)}, u32[]{:S(2)}) async-start(f32[16,64,128]{2,1,0:T(8,128)} %bitcast.7), calls=%async_computation.1 | async-start | bytes 1048576 | tf_op jit(solution)/shard_map/all_to_all | solution.py:314
  23.7 15.4 %collective-permute-start.1 = (f32[16,2,24,128]{3,2,1,0:T(8,128)S(1)}, f32[16,2,24,128]{3,2,1,0:T(8,128)S(1)}, u32[]{:S(2)}, u32[]{:S(2)}) collective-permute-start(f32[16,2,24,128]{3,2,1,0:T(8,128)S(1)} %get-tuple-element.13), channel_id=1, source_target_pairs={{0,8},{8,0},{1,9},{9,1},{2,10},{10,2},{3,11},{11,3},{4,12},{12,4},... | collective-permute-start | bytes 1179656 | tf_op jit(solution)/shard_map/ppermute | solution.py:313
  40.0 6.4 %copy-start.1 = (f32[3,2,64,64]{3,2,1,0:T(8,128)S(1)}, f32[3,2,64,64]{3,2,1,0:T(8,128)}, u32[]{:S(2)}) copy-start(f32[3,2,64,64]{3,2,1,0:T(8,128)} %param.13) | copy-start | bytes 294916
  40.0 17.2 %all-to-all-start.2 = ((f32[16,96,128]{2,1,0:T(8,128)}), f32[16,96,128]{2,1,0:T(8,128)S(1)}, u32[]{:S(2)}, u32[]{:S(2)}) async-start(f32[16,96,128]{2,1,0:T(8,128)} %bitcast.9), calls=%async_computation.2 | async-start | bytes 1572864 | tf_op jit(solution)/shard_map/all_to_all | solution.py:319
  46.4 0.9 copy-start.2
  47.5 5.3 %copy-start.6 = (s32[3]{0:T(128)S(1)}, s32[3]{0:T(128)}, u32[]{:S(2)}) copy-start(s32[3]{0:T(128)} %param.19) | copy-start | bytes 40
  47.5 5.3 %copy-start.7 = (s32[3]{0:T(128)S(1)}, s32[3]{0:T(128)}, u32[]{:S(2)}) copy-start(s32[3]{0:T(128)} %param.18) | copy-start | bytes 40
  47.5 5.3 %copy-start.8 = (s32[3]{0:T(128)S(1)}, s32[3]{0:T(128)}, u32[]{:S(2)}) copy-start(s32[3]{0:T(128)} %param.17) | copy-start | bytes 40
  47.5 9.2 %collective-permute-start = (f32[16,2,2,8,128]{4,3,2,1,0:T(8,128)S(1)}, f32[16,2,2,8,128]{4,3,2,1,0:T(8,128)S(1)}, u32[]{:S(2)}, u32[]{:S(2)}) collective-permute-start(f32[16,2,2,8,128]{4,3,2,1,0:T(8,128)S(1)} %slice.22), channel_id=1, source_target_pairs={{0,8},{8,0},{1,9},{9,1},{2,10},{10,2},{3,11},{11,3},{4,12},{12,4},... | collective-permute-start | bytes 786440 | tf_op jit(solution)/shard_map/ppermute | solution.py:317
  61.3 36.6 %collective-permute-start.2 = (f32[1024,128]{1,0:T(8,128)S(1)}, f32[1024,128]{1,0:T(8,128)S(1)}, u32[]{:S(2)}, u32[]{:S(2)}) collective-permute-start(f32[1024,128]{1,0:T(8,128)S(1)} %shard_map.119), channel_id=1, source_target_pairs={{0,4},{1,5},{2,6},{3,7},{4,0},{5,1},{6,2},{7,3},{8,12},{9,13},{10,... | collective-permute-start | bytes 1572872 | tf_op jit(solution)/shard_map/ppermute | solution.py:327

commit v5 on v4

--- a/solution.py
+++ b/solution.py
@@ -98,31 +98,17 @@
     return jnp.where(col // TOP % 3 == 1, wide - high, high).astype(BF16)
 
 
-def spread_mid(matrix):
-    row, col = iotas((MID, 4 * MID))
-    wide = hdot(matrix[:, :MID], jnp.where(row == col % MID, 1.0, 0.0))
-    row, col = iotas((4 * MID, MID))
-    pick = jnp.where(col == row % MID, 1.0, 0.0)
-    row, col = iotas((4 * MID, 4 * MID))
-    same = jnp.where(row // MID == col // MID, 1.0, 0.0)
-    return jnp.concatenate([hdot(pick, wide[:MID]) * same, hdot(pick, wide[MID:]) * same], axis=1)
-
-
 def prep_block(refs, block, slot, mid, low):
-    small_ref, large_ref, masks_ref, where_ref, built_ref = refs
+    small_ref, large_ref, masks_ref, where_ref, mid_ref, low_ref = refs
     flip, phase = masks_ref[block], masks_ref[BLOCKS + block]
     source = where_ref[0] if block == 1 else jnp.bitwise_xor(where_ref[0], where_ref[2])
     scale = sign_of(jnp.bitwise_and(source, masks_ref[2 * BLOCKS + block]))
     fold = fold_left(2 * MID, flip // LOW % MID, phase // LOW % MID)
     full = fold_right(2 * LOW, flip % LOW, phase % LOW)
-    put_pair(built_ref, slot, hdot(fold, hdot(small_ref[13 + block], mid)), hdot(hdot(low, large_ref[3 + block]), full))
+    mid_ref[slot] = three_passes([hdot(fold, hdot(small_ref[13 + block], mid))])
+    put(low_ref, slot, hdot(hdot(low, large_ref[3 + block]), full))
     fold = fold_left(2 * TOP, flip // (MID * LOW), phase // (MID * LOW))
     return hdot(fold, hdot(small_ref[8 + 2 * block], small_ref[7 + 2 * block])) * scale
-
-
-def put_pair(ref, slot, mid, low):
-    put(ref.at[:, :, : 4 * MID], slot, spread_mid(mid))
-    put(ref.at[:, :, 4 * MID :], slot, jnp.concatenate([low, times_i(low)], axis=1))
 
 
 def merged(small_ref, large_ref):
@@ -130,22 +116,16 @@
     return mid, hdot(hdot(large_ref[0], large_ref[1]), large_ref[2])
 
 
-def parts_of(ref, slot):
-    pair = ref.at[slot]
-    return tuple((pair[0, rows], pair[1, rows]) for rows in (slice(0, 4 * MID), slice(4 * MID, 8 * MID)))
-
-
-def prep_send(small_ref, large_ref, masks_ref, where_ref, high_ref, built_ref):
-    refs = (small_ref, large_ref, masks_ref, where_ref, built_ref)
-    mid, low = merged(small_ref, large_ref)
-    high_ref[...] = three_passes([prep_block(refs, slot + 1, slot, mid, low) for slot in range(2)])
-
-
-def prep_keep(small_ref, large_ref, masks_ref, where_ref, high_ref, built_ref):
-    refs = (small_ref, large_ref, masks_ref, where_ref, built_ref)
-    mid, low = merged(small_ref, large_ref)
-    high_ref[...] = three_passes([prep_block(refs, 0, 0, mid, low)])
-    put_pair(built_ref, 1, mid, low)
+def prep_send(*refs):
+    mid, low = merged(*refs[:2])
+    refs[6][...] = three_passes([prep_block(refs[:6], slot + 1, slot, mid, low) for slot in range(2)])
+
+
+def prep_keep(*refs):
+    mid, low = merged(*refs[:2])
+    refs[6][...] = three_passes([prep_block(refs[:6], 0, 0, mid, low)])
+    refs[4][1] = three_passes([mid])
+    put(refs[5], 1, low)
 
 
 def two_streams(out_ref, first, value):
@@ -183,17 +163,20 @@
 
 def low_mid(load, mid, low, store):
     for group in range(4):
-        done = dot3(split(load(group)), low)
-        same, turned = done[:, : 2 * LOW], done[:, 2 * LOW :]
-        right = jnp.concatenate(
-            [
-                jnp.concatenate([same[: 4 * MID], same[4 * MID :]], axis=1),
-                jnp.concatenate([turned[: 4 * MID], turned[4 * MID :]], axis=1),
-            ],
-            axis=0,
-        )
-        done = dot3(mid, split(right))
-        store(group, jnp.concatenate([done[:, : 2 * LOW], done[:, 2 * LOW :]], axis=0))
+        high, rest = split(dot3(split(load(group)), low))
+        values = []
+        for pair in range(4):
+            parts = [
+                jnp.concatenate([part[2 * MID * pair : 2 * MID * pair + MID], part[2 * MID * pair + MID : 2 * MID * (pair + 1)]], axis=1)
+                for part in (high, rest)
+            ]
+            total = jnp.dot(
+                mid, jnp.concatenate([parts[0], parts[0], parts[1]], axis=0), preferred_element_type=F32
+            )
+            for half in range(2):
+                part = total[:, 2 * LOW * half : 2 * LOW * (half + 1)]
+                values.append(part[:MID] + times_i(part[MID:]))
+        store(group, jnp.concatenate(values, axis=0))
 
 
 def high_step(sources, matrix_ref, out_ref):
@@ -230,21 +213,22 @@
     return store
 
 
-def send_kernel(early_ref, got_ref, late_ref, high_ref, built_ref, out_ref, first_ref, second_ref):
+def low_of(ref, slot):
+    return ref[slot, 0], ref[slot, 1]
+
+
+def send_kernel(early_ref, got_ref, late_ref, mid_ref, low_ref, high_ref, out_ref, first_ref, second_ref):
     fields = (early_ref, got_ref, late_ref)
     for slot, half_ref in enumerate((first_ref, second_ref)):
-        mid, low = parts_of(built_ref, slot)
-        low_mid(reader(fields, slot), mid, low, writer(half_ref))
+        low_mid(reader(fields, slot), mid_ref[slot], low_of(low_ref, slot), writer(half_ref))
     high_step((first_ref, second_ref), high_ref, out_ref)
 
 
-def keep_kernel(early_ref, got_ref, late_ref, high_ref, built_ref, final_ref, out_ref, first_ref):
+def keep_kernel(early_ref, got_ref, late_ref, mid_ref, low_ref, high_ref, final_ref, out_ref, first_ref):
     fields = (early_ref, got_ref, late_ref)
-    mid, low = parts_of(built_ref, 0)
-    low_mid(reader(fields, 1), mid, low, writer(first_ref))
+    low_mid(reader(fields, 1), mid_ref[0], low_of(low_ref, 0), writer(first_ref))
     high_step((first_ref,), high_ref, out_ref)
-    mid, low = parts_of(built_ref, 1)
-    low_mid(reader(fields, 0), mid, low, writer(final_ref))
+    low_mid(reader(fields, 0), mid_ref[1], low_of(low_ref, 1), writer(final_ref))
 
 
 def real_form(matrix):
@@ -319,14 +303,14 @@
     field = lax.all_to_all(
         both.reshape(XY, 4 * late, width), ("x", "y"), split_axis=0, concat_axis=0, tiled=True
     ).reshape(XY, 2, 2, late, width)
-    built = ((2, 2, 8 * MID, 256), BF16)
-    prepared = call(prep_send, 4, [((2 * TOP, 6 * TOP), BF16), built], smem=(2, 3))(small, large, masks, where)
+    built = [((2, 2 * MID, 3 * MID), BF16), ((2, 2, width, width), BF16)]
+    prepared = call(prep_send, 4, built + [((2 * TOP, 6 * TOP), BF16)], smem=(2, 3))(small, large, masks, where)
     whole = ((TOP * MID, width), F32)
     fields = (early, early_got, field)
-    (sent,) = call(send_kernel, 5, [whole], [whole, whole])(*fields, *prepared)
+    (sent,) = call(send_kernel, 6, [whole], [whole, whole])(*fields, *prepared)
     arrived = lax.ppermute(sent, "narrow", [(i, i ^ 4) for i in range(8)])
-    prepared = call(prep_keep, 4, [((2 * TOP, 3 * TOP), BF16), built], smem=(2, 3))(small, large, masks, where)
-    final, kept = call(keep_kernel, 5, [whole, whole], [whole])(*fields, *prepared)
+    prepared = call(prep_keep, 4, built + [((2 * TOP, 3 * TOP), BF16)], smem=(2, 3))(small, large, masks, where)
+    final, kept = call(keep_kernel, 6, [whole, whole], [whole])(*fields, *prepared)
     return final, kept + arrived
 
 

time: 99.7 us -> 98.3 us (0.986)
  Pallas kernels: 17.5 us -> 14.2 us
  waiting for transfers between devices: 32.1 us -> 34.2 us
    pallas_call x4, Pallas kernels: 13.8 us -> 10.5 us  [the longest x1 3.5 us: evolve(): call(keep_kernel, 6, [whole, whole], [whole])(*fields, *prepared)]
    ppermute x1, waiting for transfers between devices: 15.1 us -> 16.5 us  [evolve(): arrived = lax.ppermute(sent, 'narrow', [(i, i ^ 4) for i in range(8)])]
  transfers between devices with their start and end apart: 6 -> 6, of which waited for: 5 -> 5; matrix products, arithmetic and copies ran while one was open for 1% -> 1% of each run, Pallas kernels for 12% -> 10%
where the time goes in v5:
time: 98.3 us; the launch traced here: 97.2 us
  starting transfers between devices  44.4 us (45%)
  waiting for transfers between devices  34.2 us (35%)
  Pallas kernels  14.2 us (14%)
  local copies, waits for them, and re-layouts  2.08 us (2%)
  other arithmetic  1.48 us (2%)
    ppermute x1, waiting for transfers between devices, evolve(): arrived = lax.ppermute(sent, 'narrow', [(i, i ^ 4) for i in range(8)])  16.5 us
    ppermute x1, starting transfers between devices, evolve(): arrived = lax.ppermute(sent, 'narrow', [(i, i ^ 4) for i in range(8)])  14.6 us
    ppermute x1, waiting for transfers between devices, evolve(): got = lax.ppermute(other, 'zh', swap)  8.41 us
    all_to_all x1, starting transfers between devices, evolve(): lax.all_to_all(amplitudes.reshape(XY, 2 * MID, width), ('x', 'y'), split_...  7.72 us
    all_to_all x1, waiting for transfers between devices, evolve(): lax.all_to_all(amplitudes.reshape(XY, 2 * MID, width), ('x', 'y'), split_...  7.51 us
    ppermute x1, starting transfers between devices, evolve(): got = lax.ppermute(other, 'zh', swap)  7 us
    all_to_all x1, starting transfers between devices, evolve(): lax.all_to_all(both.reshape(XY, 4 * late, width), ('x', 'y'), split_axis=...  6.36 us
    ppermute x1, starting transfers between devices, evolve(): early_got = lax.ppermute(early[:, 2:], 'zh', swap)  5.22 us
  transfers between devices with their start and end apart: 6, of which 5 were waited for; matrix products, arithmetic and copies ran while one was open for 1% of the time, Pallas kernels for 10%

profile of v5, /device:TPU:1, one launch (start us, length us, event | category | flops | bytes accessed | tf_op | source)
XLA Modules:
  0.0 97.2 jit_solution(7635972749098720254)
XLA Ops:
  0.6 0.0 copy-start
  0.6 7.7 %all-to-all-start = ((f32[16,64,128]{2,1,0:T(8,128)}), f32[16,64,128]{2,1,0:T(8,128)S(1)}, u32[]{:S(2)}, u32[]{:S(2)}) async-start(f32[16,64,128]{2,1,0:T(8,128)} %bitcast.31), calls=%async_computation | async-start | bytes 1048576 | tf_op jit(solution)/shard_map/all_to_all | solution.py:280
  8.4 0.0 copy-done
  8.4 0.0 copy-start.3
  8.4 0.0 copy-start.4
  8.4 0.0 copy-start.5
  8.4 0.8 copy-done.3
  9.3 0.1 copy-done.4
  9.3 0.0 copy-done.5
  9.5 0.1 pad_add_fusion.where_ref.refs_3_
  9.6 0.2 maximum_maximum_fusion.small_ref.refs_0_
  9.8 1.4 %shard_map.113.top_ref = bf16[2,2,128,256]{3,2,1,0:T(8,128)(2,1)S(1)} custom-call(f32[16,64,64]{2,1,0:T(8,128)S(1)} %maximum_maximum_fusion.small_ref.refs_0_, s32[3]{0:T(128)S(1)} %pad_add_fusion.where_ref.refs_3_), custom_call_target="tpu_custom_call" | custom-call | tf_op jit(solution)/shard_map/pallas_call | solution.py:292
  11.2 7.5 %all-to-all-done = f32[16,64,128]{2,1,0:T(8,128)S(1)} async-done(((f32[16,64,128]{2,1,0:T(8,128)}), f32[16,64,128]{2,1,0:T(8,128)S(1)}, u32[]{:S(2)}, u32[]{:S(2)}) %all-to-all-start) | async-done | bytes 524320 | tf_op jit(solution)/shard_map/all_to_all | solution.py:280
  18.7 1.4 %shard_map.114 = (f32[16,2,24,128]{3,2,1,0:T(8,128)S(1)}, f32[16,2,24,128]{3,2,1,0:T(8,128)S(1)}, f32[16,4,2,8,128]{4,3,2,1,0:T(8,128)}) custom-call(f32[16,2,32,128]{3,2,1,0:T(8,128)S(1)} %bitcast.29, bf16[2,2,128,256]{3,2,1,0:T(8,128)(2,1)S(1)} %shard_map.113.top_ref), custom_call_target="tpu_custom_call" | custom-call | tf_op jit(solution)/shard_map/pallas_call | solution.py:295
  20.1 3.6 %all-to-all-start.1 = ((f32[16,64,128]{2,1,0:T(8,128)}), f32[16,64,128]{2,1,0:T(8,128)S(1)}, u32[]{:S(2)}, u32[]{:S(2)}) async-start(f32[16,64,128]{2,1,0:T(8,128)} %bitcast.7), calls=%async_computation.1 | async-start | bytes 1048576 | tf_op jit(solution)/shard_map/all_to_all | solution.py:298
  23.7 7.0 %collective-permute-start.1 = (f32[16,2,24,128]{3,2,1,0:T(8,128)S(1)}, f32[16,2,24,128]{3,2,1,0:T(8,128)S(1)}, u32[]{:S(2)}, u32[]{:S(2)}) collective-permute-start(f32[16,2,24,128]{3,2,1,0:T(8,128)S(1)} %get-tuple-element.15), channel_id=1, source_target_pairs={{0,8},{8,0},{1,9},{9,1},{2,10},{10,2},{3,11},{11,3},{4,12},{12,4},... | collective-permute-start | bytes 1179656 | tf_op jit(solution)/shard_map/ppermute | solution.py:297
  30.7 8.4 %collective-permute-done.1.got_ref = f32[16,2,24,128]{3,2,1,0:T(8,128)S(1)} collective-permute-done((f32[16,2,24,128]{3,2,1,0:T(8,128)S(1)}, f32[16,2,24,128]{3,2,1,0:T(8,128)S(1)}, u32[]{:S(2)}, u32[]{:S(2)}) %collective-permute-start.1) | collective-permute-done | bytes 393248 | tf_op jit(solution)/shard_map/ppermute | solution.py:297
  39.1 0.9 shard_map.115
  40.0 0.0 all-to-all-done.1
  40.0 0.0 copy-start.1
  40.0 6.4 %all-to-all-start.2 = ((f32[16,96,128]{2,1,0:T(8,128)}), f32[16,96,128]{2,1,0:T(8,128)S(1)}, u32[]{:S(2)}, u32[]{:S(2)}) async-start(f32[16,96,128]{2,1,0:T(8,128)} %bitcast.9), calls=%async_computation.2 | async-start | bytes 1572864 | tf_op jit(solution)/shard_map/all_to_all | solution.py:303
  46.4 0.0 copy-done.1
  46.4 0.0 copy-start.2
  46.4 0.1 copy.16
  46.5 0.8 copy-done.2
  47.3 0.1 copy.17
  47.5 0.0 copy-start.6
  47.5 0.0 copy-start.7
  47.5 0.0 copy-start.8
  47.5 5.2 %collective-permute-start = (f32[16,2,2,8,128]{4,3,2,1,0:T(8,128)S(1)}, f32[16,2,2,8,128]{4,3,2,1,0:T(8,128)S(1)}, u32[]{:S(2)}, u32[]{:S(2)}) collective-permute-start(f32[16,2,2,8,128]{4,3,2,1,0:T(8,128)S(1)} %slice.22), channel_id=1, source_target_pairs={{0,8},{8,0},{1,9},{9,1},{2,10},{10,2},{3,11},{11,3},{4,12},{12,4},... | collective-permute-start | bytes 786440 | tf_op jit(solution)/shard_map/ppermute | solution.py:301
  52.8 0.0 copy-done.6
  52.8 0.0 copy-done.7
  52.8 0.0 copy-done.8
  52.8 0.1 pad_add_fusion.1.refs_2_
  52.9 0.2 maximum_maximum_fusion.1.refs_1_
  53.0 2.4 %shard_map.118 = (bf16[2,64,96]{2,1,0:T(8,128)(2,1)S(1)}, bf16[2,2,128,128]{3,2,1,0:T(8,128)(2,1)S(1)}, bf16[64,192]{1,0:T(8,128)(2,1)S(1)}) custom-call(f32[16,64,64]{2,1,0:T(8,128)S(1)} %maximum_maximum_fusion.small_ref.refs_0_, f32[6,128,128]{2,1,0:T(8,128)S(1)} %maximum_maximum_fusion.1.refs_1_, s32[9]{0:T(128)S(1)} %pad_add_fusion.1.refs_2_, ...), custom_call_target="tpu_custom_call" | custom-call | tf_op jit(solution)/shard_map/pallas_call | solution.py:307
  55.5 1.3 %collective-permute-done.got_ref = f32[16,2,2,8,128]{4,3,2,1,0:T(8,128)S(1)} collective-permute-done((f32[16,2,2,8,128]{4,3,2,1,0:T(8,128)S(1)}, f32[16,2,2,8,128]{4,3,2,1,0:T(8,128)S(1)}, u32[]{:S(2)}, u32[]{:S(2)}) %collective-permute-start) | collective-permute-done | bytes 262176 | tf_op jit(solution)/shard_map/ppermute | solution.py:301
  56.7 0.4 all-to-all-done.2
  57.2 2.8 %shard_map.119 = f32[1024,128]{1,0:T(8,128)S(1)} custom-call(f32[16,4,2,8,128]{4,3,2,1,0:T(8,128)S(1)} %bitcast.27, f32[16,2,2,8,128]{4,3,2,1,0:T(8,128)S(1)} %collective-permute-done.got_ref, f32[16,2,2,24,128]{4,3,2,1,0:T(8,128)S(1)} %bitcast.24, bf16[2,64,96]{2,1,0:T(8,128)(2,1)S(1)} %get-tuple-element.21.mid_ref, ...), custom_call_target="tpu_custom_call" | custom-call | tf_op jit(solution)/shard_map/pallas_call | solution.py:310
  60.0 14.6 %collective-permute-start.2 = (f32[1024,128]{1,0:T(8,128)S(1)}, f32[1024,128]{1,0:T(8,128)S(1)}, u32[]{:S(2)}, u32[]{:S(2)}) collective-permute-start(f32[1024,128]{1,0:T(8,128)S(1)} %shard_map.119), channel_id=1, source_target_pairs={{0,4},{1,5},{2,6},{3,7},{4,0},{5,1},{6,2},{7,3},{8,12},{9,13},{10,... | collective-permute-start | bytes 1572872 | tf_op jit(solution)/shard_map/ppermute | solution.py:311
  74.6 1.8 %shard_map.116 = (bf16[2,64,96]{2,1,0:T(8,128)(2,1)S(1)}, bf16[2,2,128,128]{3,2,1,0:T(8,128)(2,1)S(1)}, bf16[64,96]{1,0:T(8,128)(2,1)S(1)}) custom-call(f32[16,64,64]{2,1,0:T(8,128)S(1)} %maximum_maximum_fusion.small_ref.refs_0_, f32[6,128,128]{2,1,0:T(8,128)S(1)} %maximum_maximum_fusion.1.refs_1_, s32[9]{0:T(128)S(1)} %pad_add_fusion.1.refs_2_, ...), custom_call_target="tpu_custom_call" | custom-call | tf_op jit(solution)/shard_map/pallas_call | solution.py:312
  76.4 3.5 %shard_map.117 = (f32[1024,128]{1,0:T(8,128)}, f32[1024,128]{1,0:T(8,128)S(1)}) custom-call(f32[16,4,2,8,128]{4,3,2,1,0:T(8,128)S(1)} %bitcast.28, f32[16,2,2,8,128]{4,3,2,1,0:T(8,128)S(1)} %collective-permute-done.got_ref, f32[16,2,2,24,128]{4,3,2,1,0:T(8,128)S(1)} %bitcast.25, bf16[2,64,96]{2,1,0:T(8,128)(2,1)S(1)} %get-tuple-element.16.mid_ref, ...), custom_call_target="tpu_custom_call" | custom-call | tf_op jit(solution)/shard_map/pallas_call | solution.py:313
  79.9 16.5 %collective-permute-done.2 = f32[1024,128]{1,0:T(8,128)S(1)} collective-permute-done((f32[1024,128]{1,0:T(8,128)S(1)}, f32[1024,128]{1,0:T(8,128)S(1)}, u32[]{:S(2)}, u32[]{:S(2)}) %collective-permute-start.2) | collective-permute-done | bytes 524320 | tf_op jit(solution)/shard_map/ppermute | solution.py:311
  96.4 0.8 add.15
  (7 shorter events, 0.2 us)
Async XLA Ops:
  0.6 7.7 %copy-start = (f32[3,2,2,32,32]{4,3,2,1,0:T(8,128)S(1)}, f32[3,2,2,32,32]{4,3,2,1,0:T(8,128)}, u32[]{:S(2)}) copy-start(f32[3,2,2,32,32]{4,3,2,1,0:T(8,128)} %param.14) | copy-start | bytes 147460
  0.6 18.1 %all-to-all-start = ((f32[16,64,128]{2,1,0:T(8,128)}), f32[16,64,128]{2,1,0:T(8,128)S(1)}, u32[]{:S(2)}, u32[]{:S(2)}) async-start(f32[16,64,128]{2,1,0:T(8,128)} %bitcast.31), calls=%async_computation | async-start | bytes 1048576 | tf_op jit(solution)/shard_map/all_to_all | solution.py:280
  8.4 0.9 copy-start.3
  8.4 0.9 copy-start.4
  8.4 1.0 %copy-start.5 = (f32[3,2,32,32]{3,2,1,0:T(8,128)S(1)}, f32[3,2,32,32]{3,2,1,0:T(8,128)}, u32[]{:S(2)}) copy-start(f32[3,2,32,32]{3,2,1,0:T(8,128)} %param.15) | copy-start | bytes 73732
  20.1 19.9 %all-to-all-start.1 = ((f32[16,64,128]{2,1,0:T(8,128)}), f32[16,64,128]{2,1,0:T(8,128)S(1)}, u32[]{:S(2)}, u32[]{:S(2)}) async-start(f32[16,64,128]{2,1,0:T(8,128)} %bitcast.7), calls=%async_computation.1 | async-start | bytes 1048576 | tf_op jit(solution)/shard_map/all_to_all | solution.py:298
  23.7 15.4 %collective-permute-start.1 = (f32[16,2,24,128]{3,2,1,0:T(8,128)S(1)}, f32[16,2,24,128]{3,2,1,0:T(8,128)S(1)}, u32[]{:S(2)}, u32[]{:S(2)}) collective-permute-start(f32[16,2,24,128]{3,2,1,0:T(8,128)S(1)} %get-tuple-element.15), channel_id=1, source_target_pairs={{0,8},{8,0},{1,9},{9,1},{2,10},{10,2},{3,11},{11,3},{4,12},{12,4},... | collective-permute-start | bytes 1179656 | tf_op jit(solution)/shard_map/ppermute | solution.py:297
  40.0 6.4 %copy-start.1 = (f32[3,2,64,64]{3,2,1,0:T(8,128)S(1)}, f32[3,2,64,64]{3,2,1,0:T(8,128)}, u32[]{:S(2)}) copy-start(f32[3,2,64,64]{3,2,1,0:T(8,128)} %param.13) | copy-start | bytes 294916
  40.0 17.2 %all-to-all-start.2 = ((f32[16,96,128]{2,1,0:T(8,128)}), f32[16,96,128]{2,1,0:T(8,128)S(1)}, u32[]{:S(2)}, u32[]{:S(2)}) async-start(f32[16,96,128]{2,1,0:T(8,128)} %bitcast.9), calls=%async_computation.2 | async-start | bytes 1572864 | tf_op jit(solution)/shard_map/all_to_all | solution.py:303
  46.4 0.9 copy-start.2
  47.5 5.3 %copy-start.6 = (s32[3]{0:T(128)S(1)}, s32[3]{0:T(128)}, u32[]{:S(2)}) copy-start(s32[3]{0:T(128)} %param.19) | copy-start | bytes 40
  47.5 5.3 %copy-start.7 = (s32[3]{0:T(128)S(1)}, s32[3]{0:T(128)}, u32[]{:S(2)}) copy-start(s32[3]{0:T(128)} %param.18) | copy-start | bytes 40
  47.5 5.3 %copy-start.8 = (s32[3]{0:T(128)S(1)}, s32[3]{0:T(128)}, u32[]{:S(2)}) copy-start(s32[3]{0:T(128)} %param.17) | copy-start | bytes 40
  47.5 9.2 %collective-permute-start = (f32[16,2,2,8,128]{4,3,2,1,0:T(8,128)S(1)}, f32[16,2,2,8,128]{4,3,2,1,0:T(8,128)S(1)}, u32[]{:S(2)}, u32[]{:S(2)}) collective-permute-start(f32[16,2,2,8,128]{4,3,2,1,0:T(8,128)S(1)} %slice.22), channel_id=1, source_target_pairs={{0,8},{8,0},{1,9},{9,1},{2,10},{10,2},{3,11},{11,3},{4,12},{12,4},... | collective-permute-start | bytes 786440 | tf_op jit(solution)/shard_map/ppermute | solution.py:301
  60.0 36.3 %collective-permute-start.2 = (f32[1024,128]{1,0:T(8,128)S(1)}, f32[1024,128]{1,0:T(8,128)S(1)}, u32[]{:S(2)}, u32[]{:S(2)}) collective-permute-start(f32[1024,128]{1,0:T(8,128)S(1)} %shard_map.119), channel_id=1, source_target_pairs={{0,4},{1,5},{2,6},{3,7},{4,0},{5,1},{6,2},{7,3},{8,12},{9,13},{10,... | collective-permute-start | bytes 1572872 | tf_op jit(solution)/shard_map/ppermute | solution.py:311

commit v6 on v5

--- a/solution.py
+++ b/solution.py
@@ -179,18 +179,18 @@
         store(group, jnp.concatenate(values, axis=0))
 
 
-def high_step(sources, matrix_ref, out_ref):
+def high_step(sources, matrix_ref, out_ref, first=0, items=MID):
     matrix = matrix_ref[...]
-    for item in range(0, MID, 2):
+    for item in range(0, items, 2):
         right = []
         for source_ref in sources:
-            parts = [source_ref[pl.ds(item + half, TOP, stride=MID), :] for half in range(2)]
+            parts = [source_ref[pl.ds(first + item + half, TOP, stride=MID), :] for half in range(2)]
             high, low = split(jnp.concatenate(parts, axis=1))
             right += [high, high, low]
         total = jnp.dot(matrix, jnp.concatenate(right, axis=0), preferred_element_type=F32)
         for half in range(2):
             part = total[:, 2 * LOW * half : 2 * LOW * (half + 1)]
-            out_ref[pl.ds(item + half, TOP, stride=MID), :] = part[:TOP] + times_i(part[TOP:])
+            out_ref[pl.ds(item + half, TOP, stride=items), :] = part[:TOP] + times_i(part[TOP:])
 
 
 def reader(fields, stream):
@@ -221,7 +221,11 @@
     fields = (early_ref, got_ref, late_ref)
     for slot, half_ref in enumerate((first_ref, second_ref)):
         low_mid(reader(fields, slot), mid_ref[slot], low_of(low_ref, slot), writer(half_ref))
-    high_step((first_ref, second_ref), high_ref, out_ref)
+    high_step((first_ref, second_ref), high_ref, out_ref, 0, MID // 2)
+
+
+def rest_kernel(first_ref, second_ref, high_ref, out_ref):
+    high_step((first_ref, second_ref), high_ref, out_ref, MID // 2, MID // 2)
 
 
 def keep_kernel(early_ref, got_ref, late_ref, mid_ref, low_ref, high_ref, final_ref, out_ref, first_ref):
@@ -307,11 +311,16 @@
     prepared = call(prep_send, 4, built + [((2 * TOP, 6 * TOP), BF16)], smem=(2, 3))(small, large, masks, where)
     whole = ((TOP * MID, width), F32)
     fields = (early, early_got, field)
-    (sent,) = call(send_kernel, 6, [whole], [whole, whole])(*fields, *prepared)
-    arrived = lax.ppermute(sent, "narrow", [(i, i ^ 4) for i in range(8)])
+    half = ((TOP * MID // 2, width), F32)
+    sent, *middle = call(send_kernel, 6, [half, whole, whole])(*fields, *prepared)
+    route = [(i, i ^ 4) for i in range(8)]
+    arrived = [lax.ppermute(sent, "narrow", route)]
+    (sent,) = call(rest_kernel, 3, [half])(*middle, prepared[2])
+    arrived.append(lax.ppermute(sent, "narrow", route))
     prepared = call(prep_keep, 4, built + [((2 * TOP, 3 * TOP), BF16)], smem=(2, 3))(small, large, masks, where)
     final, kept = call(keep_kernel, 6, [whole, whole], [whole])(*fields, *prepared)
-    return final, kept + arrived
+    arrived = jnp.concatenate([part.reshape(TOP, MID // 2, width) for part in arrived], axis=1)
+    return final, kept + arrived.reshape(TOP * MID, width)
 
 
 def solution(mesh):

time: 98.3 us -> 98.3 us (level)
    ppermute x1 -> x2, starting transfers between devices: 14.6 us -> 14.7 us  [the longest x1 14.6 us: evolve(): arrived.append(lax.ppermute(sent, 'narrow', route))]
    ppermute x1 -> x2, waiting for transfers between devices: 16.5 us -> 16.4 us  [the longest x1 10.8 us: evolve(): arrived.append(lax.ppermute(sent, 'narrow', route))]
    pallas_call x1 -> x2, Pallas kernels: 2.83 us -> 2.82 us  [the longest x1 2.29 us: evolve(): call(send_kernel, 6, [half, whole, whole])(*fields, *prepared)]
  transfers between devices with their start and end apart: 6 -> 7, of which waited for: 5 -> 6; matrix products, arithmetic and copies ran while one was open for 1% -> 1% of each run, Pallas kernels for 10% -> 10%
where the time goes in v6:
time: 98.3 us; the launch traced here: 97.3 us
  starting transfers between devices  44.5 us (45%)
  waiting for transfers between devices  34.1 us (35%)
  Pallas kernels  14.2 us (14%)
  local copies, waits for them, and re-layouts  2.08 us (2%)
  other arithmetic  1.53 us (2%)
    ppermute x1, starting transfers between devices, evolve(): arrived.append(lax.ppermute(sent, 'narrow', route))  14.6 us
    ppermute x1, waiting for transfers between devices, evolve(): arrived.append(lax.ppermute(sent, 'narrow', route))  10.8 us
    ppermute x1, waiting for transfers between devices, evolve(): got = lax.ppermute(other, 'zh', swap)  8.41 us
    all_to_all x1, starting transfers between devices, evolve(): lax.all_to_all(amplitudes.reshape(XY, 2 * MID, width), ('x', 'y'), split_...  7.72 us
    all_to_all x1, waiting for transfers between devices, evolve(): lax.all_to_all(amplitudes.reshape(XY, 2 * MID, width), ('x', 'y'), split_...  7.51 us
    ppermute x1, starting transfers between devices, evolve(): got = lax.ppermute(other, 'zh', swap)  7 us
    all_to_all x1, starting transfers between devices, evolve(): lax.all_to_all(both.reshape(XY, 4 * late, width), ('x', 'y'), split_axis=...  6.36 us
    ppermute x1, waiting for transfers between devices, evolve(): arrived = [lax.ppermute(sent, 'narrow', route)]  5.62 us
  transfers between devices with their start and end apart: 7, of which 6 were waited for; matrix products, arithmetic and copies ran while one was open for 1% of the time, Pallas kernels for 10%

profile of v6, /device:TPU:1, one launch (start us, length us, event | category | flops | bytes accessed | tf_op | source)
XLA Modules:
  0.0 97.3 jit_solution(10535331954594412289)
XLA Ops:
  0.6 0.0 copy-start
  0.6 7.7 %all-to-all-start = ((f32[16,64,128]{2,1,0:T(8,128)}), f32[16,64,128]{2,1,0:T(8,128)S(1)}, u32[]{:S(2)}, u32[]{:S(2)}) async-start(f32[16,64,128]{2,1,0:T(8,128)} %bitcast.35), calls=%async_computation | async-start | bytes 1048576 | tf_op jit(solution)/shard_map/all_to_all | solution.py:284
  8.4 0.0 copy-done
  8.4 0.0 copy-start.3
  8.4 0.0 copy-start.4
  8.4 0.0 copy-start.5
  8.4 0.8 copy-done.3
  9.3 0.1 copy-done.4
  9.3 0.0 copy-done.5
  9.5 0.1 pad_add_fusion.where_ref.refs_3_
  9.6 0.2 maximum_maximum_fusion.small_ref.refs_0_
  9.8 1.4 %shard_map.113.top_ref = bf16[2,2,128,256]{3,2,1,0:T(8,128)(2,1)S(1)} custom-call(f32[16,64,64]{2,1,0:T(8,128)S(1)} %maximum_maximum_fusion.small_ref.refs_0_, s32[3]{0:T(128)S(1)} %pad_add_fusion.where_ref.refs_3_), custom_call_target="tpu_custom_call" | custom-call | tf_op jit(solution)/shard_map/pallas_call | solution.py:296
  11.2 7.5 %all-to-all-done = f32[16,64,128]{2,1,0:T(8,128)S(1)} async-done(((f32[16,64,128]{2,1,0:T(8,128)}), f32[16,64,128]{2,1,0:T(8,128)S(1)}, u32[]{:S(2)}, u32[]{:S(2)}) %all-to-all-start) | async-done | bytes 524320 | tf_op jit(solution)/shard_map/all_to_all | solution.py:284
  18.7 1.4 %shard_map.114 = (f32[16,2,24,128]{3,2,1,0:T(8,128)S(1)}, f32[16,2,24,128]{3,2,1,0:T(8,128)S(1)}, f32[16,4,2,8,128]{4,3,2,1,0:T(8,128)}) custom-call(f32[16,2,32,128]{3,2,1,0:T(8,128)S(1)} %bitcast.33, bf16[2,2,128,256]{3,2,1,0:T(8,128)(2,1)S(1)} %shard_map.113.top_ref), custom_call_target="tpu_custom_call" | custom-call | tf_op jit(solution)/shard_map/pallas_call | solution.py:299
  20.1 3.6 %all-to-all-start.1 = ((f32[16,64,128]{2,1,0:T(8,128)}), f32[16,64,128]{2,1,0:T(8,128)S(1)}, u32[]{:S(2)}, u32[]{:S(2)}) async-start(f32[16,64,128]{2,1,0:T(8,128)} %bitcast.7), calls=%async_computation.1 | async-start | bytes 1048576 | tf_op jit(solution)/shard_map/all_to_all | solution.py:302
  23.7 7.0 %collective-permute-start.1 = (f32[16,2,24,128]{3,2,1,0:T(8,128)S(1)}, f32[16,2,24,128]{3,2,1,0:T(8,128)S(1)}, u32[]{:S(2)}, u32[]{:S(2)}) collective-permute-start(f32[16,2,24,128]{3,2,1,0:T(8,128)S(1)} %get-tuple-element.18), channel_id=1, source_target_pairs={{0,8},{8,0},{1,9},{9,1},{2,10},{10,2},{3,11},{11,3},{4,12},{12,4},... | collective-permute-start | bytes 1179656 | tf_op jit(solution)/shard_map/ppermute | solution.py:301
  30.7 8.4 %collective-permute-done.1.got_ref = f32[16,2,24,128]{3,2,1,0:T(8,128)S(1)} collective-permute-done((f32[16,2,24,128]{3,2,1,0:T(8,128)S(1)}, f32[16,2,24,128]{3,2,1,0:T(8,128)S(1)}, u32[]{:S(2)}, u32[]{:S(2)}) %collective-permute-start.1) | collective-permute-done | bytes 393248 | tf_op jit(solution)/shard_map/ppermute | solution.py:301
  39.1 0.9 shard_map.115
  40.0 0.0 all-to-all-done.1
  40.0 0.0 copy-start.1
  40.0 6.4 %all-to-all-start.2 = ((f32[16,96,128]{2,1,0:T(8,128)}), f32[16,96,128]{2,1,0:T(8,128)S(1)}, u32[]{:S(2)}, u32[]{:S(2)}) async-start(f32[16,96,128]{2,1,0:T(8,128)} %bitcast.9), calls=%async_computation.2 | async-start | bytes 1572864 | tf_op jit(solution)/shard_map/all_to_all | solution.py:307
  46.4 0.0 copy-done.1
  46.4 0.0 copy-start.2
  46.4 0.1 copy.16
  46.5 0.8 copy-done.2
  47.3 0.1 copy.17
  47.5 0.0 copy-start.6
  47.5 0.0 copy-start.7
  47.5 0.0 copy-start.8
  47.5 5.2 %collective-permute-start = (f32[16,2,2,8,128]{4,3,2,1,0:T(8,128)S(1)}, f32[16,2,2,8,128]{4,3,2,1,0:T(8,128)S(1)}, u32[]{:S(2)}, u32[]{:S(2)}) collective-permute-start(f32[16,2,2,8,128]{4,3,2,1,0:T(8,128)S(1)} %slice.22), channel_id=1, source_target_pairs={{0,8},{8,0},{1,9},{9,1},{2,10},{10,2},{3,11},{11,3},{4,12},{12,4},... | collective-permute-start | bytes 786440 | tf_op jit(solution)/shard_map/ppermute | solution.py:305
  52.7 0.0 copy-done.6
  52.7 0.0 copy-done.7
  52.7 0.0 copy-done.8
  52.8 0.1 pad_add_fusion.1.refs_2_
  52.9 0.2 maximum_maximum_fusion.1.refs_1_
  53.0 2.4 %shard_map.118 = (bf16[2,64,96]{2,1,0:T(8,128)(2,1)S(1)}, bf16[2,2,128,128]{3,2,1,0:T(8,128)(2,1)S(1)}, bf16[64,192]{1,0:T(8,128)(2,1)S(1)}) custom-call(f32[16,64,64]{2,1,0:T(8,128)S(1)} %maximum_maximum_fusion.small_ref.refs_0_, f32[6,128,128]{2,1,0:T(8,128)S(1)} %maximum_maximum_fusion.1.refs_1_, s32[9]{0:T(128)S(1)} %pad_add_fusion.1.refs_2_, ...), custom_call_target="tpu_custom_call" | custom-call | tf_op jit(solution)/shard_map/pallas_call | solution.py:311
  55.4 1.3 %collective-permute-done.got_ref = f32[16,2,2,8,128]{4,3,2,1,0:T(8,128)S(1)} collective-permute-done((f32[16,2,2,8,128]{4,3,2,1,0:T(8,128)S(1)}, f32[16,2,2,8,128]{4,3,2,1,0:T(8,128)S(1)}, u32[]{:S(2)}, u32[]{:S(2)}) %collective-permute-start) | collective-permute-done | bytes 262176 | tf_op jit(solution)/shard_map/ppermute | solution.py:305
  56.7 0.4 all-to-all-done.2
  57.2 2.3 %shard_map.119 = (f32[512,128]{1,0:T(8,128)S(1)}, f32[1024,128]{1,0:T(8,128)S(1)}, f32[1024,128]{1,0:T(8,128)S(1)}) custom-call(f32[16,4,2,8,128]{4,3,2,1,0:T(8,128)S(1)} %bitcast.31, f32[16,2,2,8,128]{4,3,2,1,0:T(8,128)S(1)} %collective-permute-done.got_ref, f32[16,2,2,24,128]{4,3,2,1,0:T(8,128)S(1)} %bitcast.28, ...), custom_call_target="tpu_custom_call" | custom-call | tf_op jit(solution)/shard_map/pallas_call | solution.py:315
  59.5 0.5 shard_map.120
  60.0 14.6 %collective-permute-start.3 = (f32[512,128]{1,0:T(8,128)S(1)}, f32[512,128]{1,0:T(8,128)S(1)}, u32[]{:S(2)}, u32[]{:S(2)}) collective-permute-start(f32[512,128]{1,0:T(8,128)S(1)} %shard_map.120), channel_id=1, source_target_pairs={{0,4},{1,5},{2,6},{3,7},{4,0},{5,1},{6,2},{7,3},{8,12},{9,13},{10,... | collective-permute-start | bytes 786440 | tf_op jit(solution)/shard_map/ppermute | solution.py:319
  74.6 0.1 collective-permute-start.2
  74.7 1.8 %shard_map.116 = (bf16[2,64,96]{2,1,0:T(8,128)(2,1)S(1)}, bf16[2,2,128,128]{3,2,1,0:T(8,128)(2,1)S(1)}, bf16[64,96]{1,0:T(8,128)(2,1)S(1)}) custom-call(f32[16,64,64]{2,1,0:T(8,128)S(1)} %maximum_maximum_fusion.small_ref.refs_0_, f32[6,128,128]{2,1,0:T(8,128)S(1)} %maximum_maximum_fusion.1.refs_1_, s32[9]{0:T(128)S(1)} %pad_add_fusion.1.refs_2_, ...), custom_call_target="tpu_custom_call" | custom-call | tf_op jit(solution)/shard_map/pallas_call | solution.py:320
  76.5 3.5 %shard_map.117 = (f32[1024,128]{1,0:T(8,128)}, f32[1024,128]{1,0:T(8,128)S(1)}) custom-call(f32[16,4,2,8,128]{4,3,2,1,0:T(8,128)S(1)} %bitcast.32, f32[16,2,2,8,128]{4,3,2,1,0:T(8,128)S(1)} %collective-permute-done.got_ref, f32[16,2,2,24,128]{4,3,2,1,0:T(8,128)S(1)} %bitcast.29, bf16[2,64,96]{2,1,0:T(8,128)(2,1)S(1)} %get-tuple-element.19.mid_ref, ...), custom_call_target="tpu_custom_call" | custom-call | tf_op jit(solution)/shard_map/pallas_call | solution.py:321
  80.0 10.8 %collective-permute-done.3 = f32[512,128]{1,0:T(8,128)S(1)} collective-permute-done((f32[512,128]{1,0:T(8,128)S(1)}, f32[512,128]{1,0:T(8,128)S(1)}, u32[]{:S(2)}, u32[]{:S(2)}) %collective-permute-start.3) | collective-permute-done | bytes 262176 | tf_op jit(solution)/shard_map/ppermute | solution.py:319
  90.7 5.6 %collective-permute-done.2 = f32[512,128]{1,0:T(8,128)S(1)} collective-permute-done((f32[512,128]{1,0:T(8,128)S(1)}, f32[512,128]{1,0:T(8,128)S(1)}, u32[]{:S(2)}, u32[]{:S(2)}) %collective-permute-start.2) | collective-permute-done | bytes 262176 | tf_op jit(solution)/shard_map/ppermute | solution.py:317
  96.4 0.8 bitcast_add_fusion
  (8 shorter events, 0.2 us)
Async XLA Ops:
  0.6 7.7 %copy-start = (f32[3,2,2,32,32]{4,3,2,1,0:T(8,128)S(1)}, f32[3,2,2,32,32]{4,3,2,1,0:T(8,128)}, u32[]{:S(2)}) copy-start(f32[3,2,2,32,32]{4,3,2,1,0:T(8,128)} %param.14) | copy-start | bytes 147460
  0.6 18.1 %all-to-all-start = ((f32[16,64,128]{2,1,0:T(8,128)}), f32[16,64,128]{2,1,0:T(8,128)S(1)}, u32[]{:S(2)}, u32[]{:S(2)}) async-start(f32[16,64,128]{2,1,0:T(8,128)} %bitcast.35), calls=%async_computation | async-start | bytes 1048576 | tf_op jit(solution)/shard_map/all_to_all | solution.py:284
  8.4 0.9 copy-start.3
  8.4 0.9 copy-start.4
  8.4 1.0 %copy-start.5 = (f32[3,2,32,32]{3,2,1,0:T(8,128)S(1)}, f32[3,2,32,32]{3,2,1,0:T(8,128)}, u32[]{:S(2)}) copy-start(f32[3,2,32,32]{3,2,1,0:T(8,128)} %param.15) | copy-start | bytes 73732
  20.1 19.9 %all-to-all-start.1 = ((f32[16,64,128]{2,1,0:T(8,128)}), f32[16,64,128]{2,1,0:T(8,128)S(1)}, u32[]{:S(2)}, u32[]{:S(2)}) async-start(f32[16,64,128]{2,1,0:T(8,128)} %bitcast.7), calls=%async_computation.1 | async-start | bytes 1048576 | tf_op jit(solution)/shard_map/all_to_all | solution.py:302
  23.7 15.4 %collective-permute-start.1 = (f32[16,2,24,128]{3,2,1,0:T(8,128)S(1)}, f32[16,2,24,128]{3,2,1,0:T(8,128)S(1)}, u32[]{:S(2)}, u32[]{:S(2)}) collective-permute-start(f32[16,2,24,128]{3,2,1,0:T(8,128)S(1)} %get-tuple-element.18), channel_id=1, source_target_pairs={{0,8},{8,0},{1,9},{9,1},{2,10},{10,2},{3,11},{11,3},{4,12},{12,4},... | collective-permute-start | bytes 1179656 | tf_op jit(solution)/shard_map/ppermute | solution.py:301
  40.0 6.4 %copy-start.1 = (f32[3,2,64,64]{3,2,1,0:T(8,128)S(1)}, f32[3,2,64,64]{3,2,1,0:T(8,128)}, u32[]{:S(2)}) copy-start(f32[3,2,64,64]{3,2,1,0:T(8,128)} %param.13) | copy-start | bytes 294916
  40.0 17.2 %all-to-all-start.2 = ((f32[16,96,128]{2,1,0:T(8,128)}), f32[16,96,128]{2,1,0:T(8,128)S(1)}, u32[]{:S(2)}, u32[]{:S(2)}) async-start(f32[16,96,128]{2,1,0:T(8,128)} %bitcast.9), calls=%async_computation.2 | async-start | bytes 1572864 | tf_op jit(solution)/shard_map/all_to_all | solution.py:307
  46.4 0.9 copy-start.2
  47.5 5.3 %copy-start.6 = (s32[3]{0:T(128)S(1)}, s32[3]{0:T(128)}, u32[]{:S(2)}) copy-start(s32[3]{0:T(128)} %param.19) | copy-start | bytes 40
  47.5 5.3 %copy-start.7 = (s32[3]{0:T(128)S(1)}, s32[3]{0:T(128)}, u32[]{:S(2)}) copy-start(s32[3]{0:T(128)} %param.18) | copy-start | bytes 40
  47.5 5.3 %copy-start.8 = (s32[3]{0:T(128)S(1)}, s32[3]{0:T(128)}, u32[]{:S(2)}) copy-start(s32[3]{0:T(128)} %param.17) | copy-start | bytes 40
  47.5 9.2 %collective-permute-start = (f32[16,2,2,8,128]{4,3,2,1,0:T(8,128)S(1)}, f32[16,2,2,8,128]{4,3,2,1,0:T(8,128)S(1)}, u32[]{:S(2)}, u32[]{:S(2)}) collective-permute-start(f32[16,2,2,8,128]{4,3,2,1,0:T(8,128)S(1)} %slice.22), channel_id=1, source_target_pairs={{0,8},{8,0},{1,9},{9,1},{2,10},{10,2},{3,11},{11,3},{4,12},{12,4},... | collective-permute-start | bytes 786440 | tf_op jit(solution)/shard_map/ppermute | solution.py:305
  60.0 30.7 %collective-permute-start.3 = (f32[512,128]{1,0:T(8,128)S(1)}, f32[512,128]{1,0:T(8,128)S(1)}, u32[]{:S(2)}, u32[]{:S(2)}) collective-permute-start(f32[512,128]{1,0:T(8,128)S(1)} %shard_map.120), channel_id=1, source_target_pairs={{0,4},{1,5},{2,6},{3,7},{4,0},{5,1},{6,2},{7,3},{8,12},{9,13},{10,... | collective-permute-start | bytes 786440 | tf_op jit(solution)/shard_map/ppermute | solution.py:319
  74.6 21.8 %collective-permute-start.2 = (f32[512,128]{1,0:T(8,128)S(1)}, f32[512,128]{1,0:T(8,128)S(1)}, u32[]{:S(2)}, u32[]{:S(2)}) collective-permute-start(f32[512,128]{1,0:T(8,128)S(1)} %get-tuple-element.27), channel_id=1, source_target_pairs={{0,4},{1,5},{2,6},{3,7},{4,0},{5,1},{6,2},{7,3},{8,12},{9,13},{10,... | collective-permute-start | bytes 786440 | tf_op jit(solution)/shard_map/ppermute | solution.py:317
